TPU v7x, 128 devices: a whole 4x4x4 slice. The times are simulated.
128 devices in a mesh: row: 8 (over y, core), col: 16 (over z, x).
Axes of the slice: x: 4, y: 4, z: 4, core: 2. Of those that a mesh axis runs over, the one named last changes fastest.
Arguments:
- nodes: bfloat16 [512, 512, 128], P('row', 'col'), may hold values from -6 to 6
- edges: bfloat16 [8, 16, 16, 1024, 128], P('row', 'col'), may hold values from -2000 to 2000
- senders: int32 [8, 16, 16, 1024], P('row', 'col'), may hold values from 0 to 203, as said below
- receivers: int32 [8, 16, 16, 1024], P('row', 'col'), may hold values from 0 to 127, as said below
- counts: int32 [8, 16, 16], P('row', 'col'), may hold values from 512 to 1024, as said below
- w_edge_in: bfloat16 [384, 128], replicated, may hold values from -0.3125 to 0.3125
- w_edge_hid: bfloat16 [128, 128], replicated, may hold values from -0.5 to 0.5
- w_edge_out: bfloat16 [128, 128], replicated, may hold values from -0.5 to 0.5
- edge_bias: float32 [3, 128], replicated, may hold values from -3 to 3
- edge_gain: float32 [128], replicated, may hold values from 0.25 to 1.75
- edge_shift: float32 [128], replicated, may hold values from -3 to 3
- w_node_in: bfloat16 [256, 128], replicated, may hold values from -0.375 to 0.375
- w_node_hid: bfloat16 [128, 128], replicated, may hold values from -0.5 to 0.5
- w_node_out: bfloat16 [128, 128], replicated, may hold values from -0.5 to 0.5
- node_bias: float32 [3, 128], replicated, may hold values from -3 to 3
- node_gain: float32 [128], replicated, may hold values from 0.25 to 1.75
- node_shift: float32 [128], replicated, may hold values from -3 to 3
Outputs:
- new_nodes: bfloat16 [512, 512, 128], P('row', 'col')
- new_edges: bfloat16 [8, 16, 16, 1024, 128], P('row', 'col')
Inputs may be any that keep to these rules, and one draw needn't show every extreme that they name: `senders`: the sender of slot k of band b is numbered in the window of node rows b * 4 - 1 to b * 4 + 4 and node columns -1 to 32 of its tile, row by row over 32 + 2 columns; it is one of the eight nodes around the receiver and lies inside the mesh. `receivers`: receivers are numbered row by row over the 4 x 32 nodes of the slot's band. Slots 0 to counts - 1 of a band hold edges, the others are empty; some band of every draw is full.
All inputs are finite; a program needn't handle non-finite values.
Results may differ from a plain program's by a relative error of at most 0.009.
Values may be sent and summed in bfloat16 or wider, within the bound.
A program may use at most 64 MiB of HBM per device.

v0:
```python
import jax
import jax.numpy as jnp
from jax import lax
from jax.sharding import PartitionSpec as P


def from_everyone(value, axis):
    devices = lax.axis_size(axis)
    return lax.all_to_all(
        jnp.broadcast_to(value[None], (devices, *value.shape)), axis, 0, 0, tiled=True
    )


def over_copies(value, axis):
    everything = from_everyone(value, axis)
    return jnp.sum(everything, axis=0)


def in_one(arrays, axis):
    ends = [0]
    for a in arrays:
        ends.append(ends[-1] + a.size)
    total = over_copies(jnp.concatenate([a.ravel() for a in arrays]), axis)
    return tuple((total[b:e].reshape(a.shape) for a, b, e in zip(arrays, ends, ends[1:])))


def extended(value, sides, width):
    for axis, dim in sides:
        devices, length = (lax.axis_size(axis), value.shape[dim])
        up = [(i, (i + 1) % devices) for i in range(devices - 1)]
        down = [(j, i) for i, j in up]
        last = lax.slice_in_dim(value, length - width, length, axis=dim)
        first = lax.slice_in_dim(value, 0, width, axis=dim)
        before = lax.ppermute(last, axis, up)
        after = lax.ppermute(first, axis, down)
        value = jnp.concatenate([before, value, after], axis=dim)
    return value


def layer_norm(values):
    centred = values - jnp.mean(values, axis=-1, keepdims=True)
    spread = jnp.mean(centred * centred, axis=-1, keepdims=True)
    return centred * lax.rsqrt(spread + 1e-05)


def per_device(
    nodes,
    edges,
    senders,
    receivers,
    counts,
    w_edge_in,
    w_edge_hid,
    w_edge_out,
    edge_bias,
    edge_gain,
    edge_shift,
    w_node_in,
    w_node_hid,
    w_node_out,
    node_bias,
    node_gain,
    node_shift,
):
    rows_tile, cols_tile, latent = nodes.shape
    num_bands = edges.shape[2]
    slot_count = edges.shape[3]
    band_rows = rows_tile // num_bands
    tile_edges = edges[0, 0]
    tile_send = senders[0, 0]
    tile_recv = receivers[0, 0]
    tile_counts = counts[0, 0]
    live_mask = (
        lax.broadcasted_iota(jnp.int32, (num_bands, slot_count), 1) < tile_counts[:, None]
    ).astype(jnp.float32)
    local_count = jnp.sum(tile_counts).astype(jnp.float32)
    values = tile_edges.astype(jnp.float32)
    weighted = values * live_mask[..., None]
    local_sum = jnp.sum(weighted, axis=(0, 1))
    local_power = jnp.sum(weighted * values, axis=(0, 1))
    row_count, row_sum, row_power = in_one((local_count, local_sum, local_power), "col")
    edge_total, summed, power = in_one((row_count, row_sum, row_power), "row")
    edge_mean = summed / edge_total
    edge_var = power / edge_total - edge_mean * edge_mean
    inv_spread = lax.rsqrt(edge_var + 1e-05)
    padded = extended(nodes, (("row", 0), ("col", 1)), 1)
    window_rows = band_rows + 2
    send_columns = lax.broadcasted_iota(jnp.int32, (1, window_rows * (cols_tile + 2)), 1)
    recv_columns = lax.broadcasted_iota(jnp.int32, (1, band_rows * cols_tile), 1)

    def band_step(inputs):
        band_index, edge_block, send_index, recv_index, band_live = inputs
        start_row = band_index * band_rows
        window = lax.dynamic_slice_in_dim(padded, start_row, window_rows, 0).reshape(-1, latent)
        own_nodes = lax.dynamic_slice_in_dim(nodes, start_row, band_rows, 0).reshape(-1, latent)
        pick_send = (send_index[:, None] == send_columns).astype(jnp.bfloat16)
        pick_recv = (recv_index[:, None] == recv_columns).astype(jnp.bfloat16)
        sender_lat = jnp.dot(pick_send, window, preferred_element_type=jnp.float32).astype(
            jnp.bfloat16
        )
        receiver_lat = jnp.dot(pick_recv, own_nodes, preferred_element_type=jnp.float32).astype(
            jnp.bfloat16
        )
        normed = ((edge_block.astype(jnp.float32) - edge_mean) * inv_spread).astype(jnp.bfloat16)
        joined = jnp.concatenate([normed, sender_lat, receiver_lat], axis=1)
        hidden_one = jax.nn.relu(
            jnp.dot(joined, w_edge_in, preferred_element_type=jnp.float32) + edge_bias[0]
        ).astype(jnp.bfloat16)
        hidden_two = jax.nn.relu(
            jnp.dot(hidden_one, w_edge_hid, preferred_element_type=jnp.float32) + edge_bias[1]
        ).astype(jnp.bfloat16)
        message = jnp.dot(hidden_two, w_edge_out, preferred_element_type=jnp.float32) + edge_bias[2]
        fresh = (
            band_live[:, None]
            * (normed.astype(jnp.float32) + layer_norm(message) * edge_gain + edge_shift)
        ).astype(jnp.bfloat16)
        summed_band = lax.dot_general(
            pick_recv, fresh, (((0,), (0,)), ((), ())), preferred_element_type=jnp.float32
        )
        return (fresh, summed_band)

    band_ids = jnp.arange(num_bands, dtype=jnp.int32)
    fresh_edges, band_sums = lax.map(
        band_step, (band_ids, tile_edges, tile_send, tile_recv, live_mask)
    )
    gathered = band_sums.reshape(rows_tile * cols_tile, latent).astype(jnp.bfloat16)
    own_flat = nodes.reshape(rows_tile * cols_tile, latent)
    node_input = jnp.concatenate([own_flat, gathered], axis=1)
    node_one = jax.nn.relu(
        jnp.dot(node_input, w_node_in, preferred_element_type=jnp.float32) + node_bias[0]
    ).astype(jnp.bfloat16)
    node_two = jax.nn.relu(
        jnp.dot(node_one, w_node_hid, preferred_element_type=jnp.float32) + node_bias[1]
    ).astype(jnp.bfloat16)
    node_message = jnp.dot(node_two, w_node_out, preferred_element_type=jnp.float32) + node_bias[2]
    updated = (
        own_flat.astype(jnp.float32) + layer_norm(node_message) * node_gain + node_shift
    ).astype(jnp.bfloat16)
    return (updated.reshape(rows_tile, cols_tile, latent), fresh_edges[None, None])


def solution(mesh):
    in_specs = (
        P("row", "col", None),
        P("row", "col", None, None, None),
        P("row", "col", None, None),
        P("row", "col", None, None),
        P("row", "col", None),
        P(),
        P(),
        P(),
        P(),
        P(),
        P(),
        P(),
        P(),
        P(),
        P(),
        P(),
        P(),
    )
    out_specs = (P("row", "col", None), P("row", "col", None, None, None))
    return jax.shard_map(
        per_device, mesh=mesh, in_specs=in_specs, out_specs=out_specs, check_vma=False
    )
```

profile of v0, /device:TPU:14, one launch (start us, length us, event | category | flops | bytes accessed | tf_op | source)
XLA Modules:
  0.0 179.3 jit_solution(11689584861741269186)
XLA Ops:
  1.4 1.9 %collective-permute-start.1 = (bf16[1,32,128]{2,1,0:T(8,128)(2,1)S(1)}, bf16[1,32,128]{2,1,0:T(8,128)(2,1)S(1)}, u32[]{:S(2)}, u32[]{:S(2)}) collective-permute-start(bf16[1,32,128]{2,1,0:T(8,128)(2,1)S(1)} %get-tuple-element.195), channel_id=1, source_target_pairs={{16,0},{32,16},{48,32},{64,48},{80,64},{96,80},{112,96},{17,1},{33... | collective-permute-start | bytes 24584 | tf_op jit(solution)/shard_map/ppermute | solution.py:35
  3.3 2.4 %collective-permute-start = (bf16[1,32,128]{2,1,0:T(8,128)(2,1)S(1)}, bf16[1,32,128]{2,1,0:T(8,128)(2,1)S(1)}, u32[]{:S(2)}, u32[]{:S(2)}) collective-permute-start(bf16[1,32,128]{2,1,0:T(8,128)(2,1)S(1)} %get-tuple-element.196), channel_id=1, source_target_pairs={{0,16},{16,32},{32,48},{48,64},{64,80},{80,96},{96,112},{1,17},{17... | collective-permute-start | bytes 24584 | tf_op jit(solution)/shard_map/ppermute | solution.py:34
  5.7 1.3 reduce_sum.81
  8.4 6.4 %copy.23 = bf16[1,1,16,1024,128]{3,4,2,1,0:T(8,128)(2,1)} copy(bf16[1,1,16,1024,128]{4,3,2,1,0:T(8,128)(2,1)} %param.20) | data formatting | bytes 8388608 | tf_op args[1]
  14.9 4.8 %multiply_reduce_fusion.1 = (f32[128]{0:T(128)S(1)}, f32[128]{0:T(128)S(1)}) fusion(f32[16,1024]{1,0:T(8,128)S(1)} %fusion.44, bf16[1,1,16,1024,128]{3,4,2,1,0:T(8,128)(2,1)} %copy.23), kind=kLoop, calls=%fused_computation.45 | loop fusion | flops 10485504 | bytes 4260864 | tf_op jit(solution)/shard_map/reduce_sum | solution.py:79
  20.4 8.3 %all-to-all-start = ((f32[16,1,257]{2,1,0:T(1,128)}), f32[16,1,257]{2,1,0:T(1,128)S(1)}, u32[]{:S(2)}, u32[]{:S(2)}) async-start(f32[16,1,257]{2,1,0:T(1,128)} %broadcast_in_dim.18), calls=%async_computation | async-start | bytes 49152 | tf_op jit(solution)/shard_map/all_to_all | solution.py:9
  28.8 5.5 %all-to-all-done = f32[16,1,257]{2,1,0:T(1,128)S(1)} async-done(((f32[16,1,257]{2,1,0:T(1,128)}), f32[16,1,257]{2,1,0:T(1,128)S(1)}, u32[]{:S(2)}, u32[]{:S(2)}) %all-to-all-start) | async-done | bytes 16480 | tf_op jit(solution)/shard_map/all_to_all | solution.py:9
  35.0 4.9 %all-to-all-start.1 = ((f32[8,1,257]{2,1,0:T(1,128)}), f32[8,1,257]{2,1,0:T(1,128)S(1)}, u32[]{:S(2)}, u32[]{:S(2)}) async-start(f32[8,1,257]{2,1,0:T(1,128)} %broadcast_in_dim.19), calls=%async_computation.1 | async-start | bytes 24576 | tf_op jit(solution)/shard_map/all_to_all | solution.py:9
  39.9 4.0 %collective-permute-start.2 = (bf16[66,1,128]{2,1,0:T(2,128)(2,1)S(1)}, bf16[66,1,128]{2,1,0:T(2,128)(2,1)S(1)}, u32[]{:S(2)}, u32[]{:S(2)}) collective-permute-start(bf16[66,1,128]{2,1,0:T(2,128)(2,1)S(1)} %get-tuple-element.193), channel_id=1, source_target_pairs={{0,1},{1,2},{2,3},{3,4},{4,5},{5,6},{6,7},{7,8},{8,9},{9,10},{10,1... | collective-permute-start | bytes 50696 | tf_op jit(solution)/shard_map/ppermute | solution.py:34
  43.9 1.9 %collective-permute-start.3 = (bf16[66,1,128]{2,1,0:T(2,128)(2,1)S(1)}, bf16[66,1,128]{2,1,0:T(2,128)(2,1)S(1)}, u32[]{:S(2)}, u32[]{:S(2)}) collective-permute-start(bf16[66,1,128]{2,1,0:T(2,128)(2,1)S(1)} %get-tuple-element.194), channel_id=1, source_target_pairs={{1,0},{2,1},{3,2},{4,3},{5,4},{6,5},{7,6},{8,7},{9,8},{10,9},{11,1... | collective-permute-start | bytes 50696 | tf_op jit(solution)/shard_map/ppermute | solution.py:35
  47.1 4.7 %collective-permute-done.3 = bf16[66,1,128]{2,1,0:T(2,128)(2,1)S(1)} collective-permute-done((bf16[66,1,128]{2,1,0:T(2,128)(2,1)S(1)}, bf16[66,1,128]{2,1,0:T(2,128)(2,1)S(1)}, u32[]{:S(2)}, u32[]{:S(2)}) %collective-permute-start.3) | collective-permute-done | bytes 16928 | tf_op jit(solution)/shard_map/ppermute | solution.py:35
  52.3 123.6 %while.13 = (s32[]{:T(128)}, bf16[16,1024,128]{2,1,0:T(8,128)(2,1)}, bf16[16,128,128]{2,1,0:T(8,128)(2,1)S(1)}, f32[16,1024]{1,0:T(8,128)S(1)}, bf16[16,1024,128...) while((s32[]{:T(128)}, ...), condition=%wide.region_8.9_spmd.clone, body=%wide.region_5.8_spmd.clone.sunk | while | flops 295121920 | bytes 6441800 | solution.py:123
  55.3 1.2 fusion.85
  57.5 1.2 multiply_convert_fusion.2
  61.3 0.8 constant_dynamic-slice_fusion.10
  63.1 1.2 fusion.85
  65.2 1.2 multiply_convert_fusion.2
  70.8 1.2 fusion.85
  72.9 1.2 multiply_convert_fusion.2
  78.5 1.2 fusion.85
  80.6 1.2 multiply_convert_fusion.2
  86.2 1.2 fusion.85
  88.4 1.2 multiply_convert_fusion.2
  92.2 0.8 constant_dynamic-slice_fusion.10
  93.9 1.2 fusion.85
  96.1 1.2 multiply_convert_fusion.2
  101.7 1.2 fusion.85
  103.8 1.2 multiply_convert_fusion.2
  109.4 1.2 fusion.85
  111.5 1.2 multiply_convert_fusion.2
  115.4 0.8 constant_dynamic-slice_fusion.10
  117.1 1.2 fusion.85
  119.2 1.2 multiply_convert_fusion.2
  124.8 1.2 fusion.85
  127.0 1.2 multiply_convert_fusion.2
  132.6 1.2 fusion.85
  134.7 1.2 multiply_convert_fusion.2
  140.3 1.2 fusion.85
  142.4 1.2 multiply_convert_fusion.2
  148.0 1.2 fusion.85
  150.1 1.2 multiply_convert_fusion.2
  155.7 1.2 fusion.85
  157.9 1.2 multiply_convert_fusion.2
  163.4 1.2 fusion.85
  165.6 1.2 multiply_convert_fusion.2
  171.2 1.2 fusion.85
  173.3 1.2 multiply_convert_fusion.2
  177.9 1.5 add_convert_fusion
  (322 shorter events, 77.5 us)
Async XLA Ops:
  0.6 175.2 %copy-start = (bf16[256,128]{1,0:T(8,128)(2,1)S(1)}, bf16[256,128]{1,0:T(8,128)(2,1)}, u32[]{:S(2)}) copy-start(bf16[256,128]{1,0:T(8,128)(2,1)} %param.30) | copy-start | bytes 196612
  1.4 27.4 %collective-permute-start.1 = (bf16[1,32,128]{2,1,0:T(8,128)(2,1)S(1)}, bf16[1,32,128]{2,1,0:T(8,128)(2,1)S(1)}, u32[]{:S(2)}, u32[]{:S(2)}) collective-permute-start(bf16[1,32,128]{2,1,0:T(8,128)(2,1)S(1)} %get-tuple-element.195), channel_id=1, source_target_pairs={{16,0},{32,16},{48,32},{64,48},{80,64},{96,80},{112,96},{17,1},{33... | collective-permute-start | bytes 24584 | tf_op jit(solution)/shard_map/ppermute | solution.py:35
  3.3 25.4 %collective-permute-start = (bf16[1,32,128]{2,1,0:T(8,128)(2,1)S(1)}, bf16[1,32,128]{2,1,0:T(8,128)(2,1)S(1)}, u32[]{:S(2)}, u32[]{:S(2)}) collective-permute-start(bf16[1,32,128]{2,1,0:T(8,128)(2,1)S(1)} %get-tuple-element.196), channel_id=1, source_target_pairs={{0,16},{16,32},{32,48},{48,64},{64,80},{80,96},{96,112},{1,17},{17... | collective-permute-start | bytes 24584 | tf_op jit(solution)/shard_map/ppermute | solution.py:34
  14.8 13.9 %copy-start.7 = (f32[3,128]{1,0:T(4,128)S(1)}, f32[3,128]{1,0:T(4,128)}, u32[]{:S(2)}) copy-start(f32[3,128]{1,0:T(4,128)} %param.33) | copy-start | bytes 4612
  14.8 13.9 %copy-start.1 = (bf16[64,32,128]{2,1,0:T(8,128)(2,1)S(1)}, bf16[64,32,128]{2,1,0:T(8,128)(2,1)}, u32[]{:S(2)}) copy-start(bf16[64,32,128]{2,1,0:T(8,128)(2,1)} %param.19) | copy-start | bytes 1572868
  14.8 37.4 %copy-start.2 = (bf16[128,128]{1,0:T(8,128)(2,1)S(1)}, bf16[128,128]{1,0:T(8,128)(2,1)}, u32[]{:S(2)}) copy-start(bf16[128,128]{1,0:T(8,128)(2,1)} %param.26) | copy-start | bytes 98308
  14.8 37.4 %copy-start.4 = (f32[3,128]{1,0:T(4,128)S(1)}, f32[3,128]{1,0:T(4,128)}, u32[]{:S(2)}) copy-start(f32[3,128]{1,0:T(4,128)} %param.27) | copy-start | bytes 4612
  14.8 37.4 %copy-start.5 = (f32[128]{0:T(128)S(1)}, f32[128]{0:T(128)}, u32[]{:S(2)}) copy-start(f32[128]{0:T(128)} %param.28) | copy-start | bytes 1540
  14.8 37.4 %copy-start.6 = (f32[128]{0:T(128)S(1)}, f32[128]{0:T(128)}, u32[]{:S(2)}) copy-start(f32[128]{0:T(128)} %param.29) | copy-start | bytes 1540
  14.8 37.4 %copy-start.10 = (bf16[384,128]{1,0:T(8,128)(2,1)S(1)}, bf16[384,128]{1,0:T(8,128)(2,1)}, u32[]{:S(2)}) copy-start(bf16[384,128]{1,0:T(8,128)(2,1)} %param.24) | copy-start | bytes 294916
  14.8 37.4 %copy-start.11 = (bf16[128,128]{1,0:T(8,128)(2,1)S(1)}, bf16[128,128]{1,0:T(8,128)(2,1)}, u32[]{:S(2)}) copy-start(bf16[128,128]{1,0:T(8,128)(2,1)} %param.25) | copy-start | bytes 98308
  20.4 13.9 %all-to-all-start = ((f32[16,1,257]{2,1,0:T(1,128)}), f32[16,1,257]{2,1,0:T(1,128)S(1)}, u32[]{:S(2)}, u32[]{:S(2)}) async-start(f32[16,1,257]{2,1,0:T(1,128)} %broadcast_in_dim.18), calls=%async_computation | async-start | bytes 49152 | tf_op jit(solution)/shard_map/all_to_all | solution.py:9
  35.0 10.8 %all-to-all-start.1 = ((f32[8,1,257]{2,1,0:T(1,128)}), f32[8,1,257]{2,1,0:T(1,128)S(1)}, u32[]{:S(2)}, u32[]{:S(2)}) async-start(f32[8,1,257]{2,1,0:T(1,128)} %broadcast_in_dim.19), calls=%async_computation.1 | async-start | bytes 24576 | tf_op jit(solution)/shard_map/all_to_all | solution.py:9
  39.9 7.2 %collective-permute-start.2 = (bf16[66,1,128]{2,1,0:T(2,128)(2,1)S(1)}, bf16[66,1,128]{2,1,0:T(2,128)(2,1)S(1)}, u32[]{:S(2)}, u32[]{:S(2)}) collective-permute-start(bf16[66,1,128]{2,1,0:T(2,128)(2,1)S(1)} %get-tuple-element.193), channel_id=1, source_target_pairs={{0,1},{1,2},{2,3},{3,4},{4,5},{5,6},{6,7},{7,8},{8,9},{9,10},{10,1... | collective-permute-start | bytes 50696 | tf_op jit(solution)/shard_map/ppermute | solution.py:34
  43.9 7.9 %collective-permute-start.3 = (bf16[66,1,128]{2,1,0:T(2,128)(2,1)S(1)}, bf16[66,1,128]{2,1,0:T(2,128)(2,1)S(1)}, u32[]{:S(2)}, u32[]{:S(2)}) collective-permute-start(bf16[66,1,128]{2,1,0:T(2,128)(2,1)S(1)} %get-tuple-element.194), channel_id=1, source_target_pairs={{1,0},{2,1},{3,2},{4,3},{5,4},{6,5},{7,6},{8,7},{9,8},{10,9},{11,1... | collective-permute-start | bytes 50696 | tf_op jit(solution)/shard_map/ppermute | solution.py:35
  52.3 123.6 %copy-start.12 = (bf16[128,128]{1,0:T(8,128)(2,1)S(1)}, bf16[128,128]{1,0:T(8,128)(2,1)}, u32[]{:S(2)}) copy-start(bf16[128,128]{1,0:T(8,128)(2,1)} %param.31) | copy-start | bytes 98308
  52.3 124.4 %copy-start.3 = (bf16[128,128]{1,0:T(8,128)(2,1)S(1)}, bf16[128,128]{1,0:T(8,128)(2,1)}, u32[]{:S(2)}) copy-start(bf16[128,128]{1,0:T(8,128)(2,1)} %param.32) | copy-start | bytes 98308
  175.9 2.0 %copy-start.8 = (f32[128]{0:T(128)S(1)}, f32[128]{0:T(128)}, u32[]{:S(2)}) copy-start(f32[128]{0:T(128)} %param.35) | copy-start | bytes 1540
  175.9 2.0 %copy-start.9 = (f32[128]{0:T(128)S(1)}, f32[128]{0:T(128)}, u32[]{:S(2)}) copy-start(f32[128]{0:T(128)} %param.34) | copy-start | bytes 1540
where the time goes:
time: 182 us; the launch traced here: 179 us
  other arithmetic  49.4 us (27%)
  local copies, waits for them, and re-layouts  46.4 us (25%)
  matrix products  36 us (20%)
  starting transfers between devices  23.3 us (13%)
  loops' own time  12.4 us (7%)
  waiting for transfers between devices  10.2 us (6%)
    dynamic_slice x48, local copies, waits for them, and re-layouts, per_device(): lax.map(band_step, (band_ids, tile_edges, tile_send, tile_recv, live_mask))  22.2 us
    convert_element_type x16, other arithmetic, band_step(): fresh = (band_live[:, None] * (normed.astype(jnp.float32) + layer_norm(me...  19.3 us
    convert_element_type x16, other arithmetic, band_step(): ((edge_block.astype(jnp.float32) - edge_mean) * inv_spread).astype(jnp.bf...  18.6 us
    dynamic_update_slice x32, local copies, waits for them, and re-layouts, per_device(): lax.map(band_step, (band_ids, tile_edges, tile_send, tile_recv, live_mask))  14.3 us
    all_to_all x2, starting transfers between devices, from_everyone(): lax.all_to_all(jnp.broadcast_to(value[None], (devices, *value.shape)), ax...  13.1 us
    another operation x1, loops' own time, per_device(): lax.map(band_step, (band_ids, tile_edges, tile_send, tile_recv, live_mask))  12.4 us
    dot_general x16, matrix products, band_step(): jnp.dot(hidden_one, w_edge_hid, preferred_element_type=jnp.float32)  9.19 us
    dot_general x16, matrix products, band_step(): jnp.dot(pick_send, window, preferred_element_type=jnp.float32)  7.49 us
  transfers between devices with their start and end apart: 6, of which 2 were waited for; matrix products, arithmetic and copies ran while one was open for 9% of the time, Pallas kernels for 0%

commit v1 on v0

v1 whole, which is shorter than its diff:
```python
import functools

import jax
import jax.numpy as jnp
from jax import lax
from jax.experimental import pallas as pl
from jax.experimental.pallas import tpu as pltpu
from jax.sharding import PartitionSpec as P

F32 = jnp.float32
BF16 = jnp.bfloat16
LAT = 128
ROWS = 64
COLS = 32
BANDS = 16
SLOTS = 1024
BAND_NODES = 128
BLK = 256
HALF = BLK // 2
NBLK = SLOTS // BLK
NB = 2
RING = 8
STAGES = 5
TRASH = BANDS * NBLK
WORK = TRASH + NB * (STAGES + 2)
EPS = 1e-5
MESH = pl.DeviceIdType.MESH


def combine(parts):
    n = functools.reduce(jnp.add, [p[0:1] for p in parts])
    weighted = functools.reduce(jnp.add, [p[0:1] * p[1:2] for p in parts])
    mean = weighted / n
    m2 = None
    for p in parts:
        d = p[1:2] - mean
        t = p[2:3] + p[0:1] * d * d
        m2 = t if m2 is None else m2 + t
    return n, mean, m2


def comm_kernel(
    nodes_hbm, edges_hbm, counts, stats_out, halo_out,
    nodes_v, edges_v, cols_v, halo_v, mine1, mine2, got1, got2,
    edge_sem, node_sem, hs_sem, hr_sem, s1_sem, r1_sem, s2_sem, r2_sem,
):
    n_row, n_col = lax.axis_size("row"), lax.axis_size("col")
    row, col = lax.axis_index("row"), lax.axis_index("col")
    up, down = lax.rem(row + n_row - 1, n_row), lax.rem(row + 1, n_row)
    left, right = lax.rem(col + n_col - 1, n_col), lax.rem(col + 1, n_col)

    node_copy = pltpu.make_async_copy(nodes_hbm, nodes_v, node_sem)
    node_copy.start()
    edge_copies = []
    for b in range(BANDS):
        c = pltpu.make_async_copy(
            edges_hbm.at[pl.ds(b * SLOTS, SLOTS)], edges_v.at[pl.ds(b * SLOTS, SLOTS)], edge_sem.at[b]
        )
        c.start()
        edge_copies.append(c)

    barrier = pltpu.get_barrier_semaphore()
    peers = [(row, lax.rem(col + k, n_col)) for k in range(1, n_col)]
    peers += [(lax.rem(row + k, n_row), col) for k in range(1, n_row)]
    peers += [(up, left), (up, right), (down, left), (down, right)]
    for p in peers:
        pl.semaphore_signal(barrier, inc=1, device_id=p, device_id_type=MESH)

    node_copy.wait()
    cols_v[0] = nodes_v[:, 0, :]
    cols_v[1] = nodes_v[:, COLS - 1, :]
    pl.semaphore_wait(barrier, len(peers))

    sends = [
        (nodes_v.at[ROWS - 1], (0, 32), (down, col)),
        (nodes_v.at[0], (32, 32), (up, col)),
        (cols_v.at[1], (64, 64), (row, right)),
        (cols_v.at[0], (128, 64), (row, left)),
        (cols_v.at[1, pl.ds(48, 16)], (192, 16), (down, right)),
        (cols_v.at[0, pl.ds(48, 16)], (208, 16), (down, left)),
        (cols_v.at[1, pl.ds(0, 16)], (224, 16), (up, right)),
        (cols_v.at[0, pl.ds(0, 16)], (240, 16), (up, left)),
    ]
    halo_copies = []
    for k, (src, (start, size), dev) in enumerate(sends):
        c = pltpu.make_async_remote_copy(
            src_ref=src, dst_ref=halo_v.at[pl.ds(start, size)],
            send_sem=hs_sem.at[k], recv_sem=hr_sem.at[k], device_id=dev, device_id_type=MESH,
        )
        c.start()
        halo_copies.append(c)

    edge_copies[0].wait()
    pivot = edges_v[0:16, :].astype(F32)[0:1]
    slot_id = lax.broadcasted_iota(jnp.int32, (64, LAT), 0)

    def band_stats(b, carry):
        s, q = carry
        pltpu.make_async_copy(
            edges_hbm.at[pl.ds(b * SLOTS, SLOTS)], edges_v.at[pl.ds(b * SLOTS, SLOTS)], edge_sem.at[b]
        ).wait()
        return band_sums(b, s, q)

    def band_sums(b, s, q):
        count = counts[0, b]
        for j in range(SLOTS // 64):
            d = edges_v[pl.ds(pl.multiple_of(b * SLOTS + j * 64, 64), 64), :].astype(F32) - pivot
            if j >= SLOTS // 128:
                d = jnp.where(slot_id < count - j * 64, d, 0.0)
            e = d * d
            s = s + ((d[0:8] + d[8:16]) + (d[16:24] + d[24:32])) + ((d[32:40] + d[40:48]) + (d[48:56] + d[56:64]))
            q = q + ((e[0:8] + e[8:16]) + (e[16:24] + e[24:32])) + ((e[32:40] + e[40:48]) + (e[48:56] + e[56:64]))
        return s, q

    zero = jnp.zeros((8, LAT), F32)
    s, q = band_sums(0, zero, zero)
    s, q = lax.fori_loop(1, BANDS, band_stats, (s, q))
    total = counts[0, 0]
    for b in range(1, BANDS):
        total = total + counts[0, b]
    n = jnp.full((1, LAT), total.astype(F32))
    s = jnp.sum(s, axis=0, keepdims=True)
    q = jnp.sum(q, axis=0, keepdims=True)
    local_mean = s / n
    filler = jnp.zeros((5, LAT), F32)
    mine1[...] = jnp.concatenate([n, pivot + local_mean, q - s * local_mean, filler], axis=0)

    copies = []
    for k in range(1, n_col):
        c = pltpu.make_async_remote_copy(
            src_ref=mine1, dst_ref=got1.at[k], send_sem=s1_sem.at[k], recv_sem=r1_sem.at[k],
            device_id=(row, lax.rem(col + k, n_col)), device_id_type=MESH,
        )
        c.start()
        copies.append(c)
    for c in copies:
        c.wait_recv()
    n, mean, m2 = combine([mine1[...]] + [got1[k] for k in range(1, n_col)])
    mine2[...] = jnp.concatenate([n, mean, m2, filler], axis=0)
    copies2 = []
    for k in range(1, n_row):
        c = pltpu.make_async_remote_copy(
            src_ref=mine2, dst_ref=got2.at[k], send_sem=s2_sem.at[k], recv_sem=r2_sem.at[k],
            device_id=(lax.rem(row + k, n_row), col), device_id_type=MESH,
        )
        c.start()
        copies2.append(c)
    for c in halo_copies:
        c.wait_recv()
    halo_out[...] = halo_v[...]
    for c in copies2:
        c.wait_recv()
    n, mean, m2 = combine([mine2[...]] + [got2[k] for k in range(1, n_row)])
    inv = lax.rsqrt(m2 / n + EPS)
    stats_out[...] = jnp.concatenate([mean, inv, jnp.zeros((6, LAT), F32)], axis=0)
    for c in halo_copies + copies + copies2:
        c.wait_send()


def communicate(nodes, edges, counts):
    n_row, n_col = lax.axis_size("row"), lax.axis_size("col")
    any_spec = pl.BlockSpec(memory_space=pl.ANY)
    return pl.pallas_call(
        comm_kernel,
        out_shape=(jax.ShapeDtypeStruct((8, LAT), F32), jax.ShapeDtypeStruct((256, LAT), BF16)),
        in_specs=[any_spec, any_spec, pl.BlockSpec(memory_space=pltpu.SMEM)],
        out_specs=(pl.BlockSpec(memory_space=pltpu.VMEM), pl.BlockSpec(memory_space=pltpu.VMEM)),
        scratch_shapes=[
            pltpu.VMEM((ROWS, COLS, LAT), BF16),
            pltpu.VMEM((BANDS * SLOTS, LAT), BF16),
            pltpu.VMEM((2, ROWS, LAT), BF16),
            pltpu.VMEM((256, LAT), BF16),
            pltpu.VMEM((8, LAT), F32),
            pltpu.VMEM((8, LAT), F32),
            pltpu.VMEM((n_col, 8, LAT), F32),
            pltpu.VMEM((n_row, 8, LAT), F32),
            pltpu.SemaphoreType.DMA((BANDS,)),
            pltpu.SemaphoreType.DMA,
            pltpu.SemaphoreType.DMA((8,)),
            pltpu.SemaphoreType.DMA((8,)),
            pltpu.SemaphoreType.DMA((n_col,)),
            pltpu.SemaphoreType.DMA((n_col,)),
            pltpu.SemaphoreType.DMA((n_row,)),
            pltpu.SemaphoreType.DMA((n_row,)),
        ],
        compiler_params=pltpu.CompilerParams(collective_id=0, has_side_effects=True),
        name="exchange",
    )(nodes, edges, counts)


def dot(a, b):
    return jnp.dot(a, b, preferred_element_type=F32)


def block_diagonal(w):
    z = jnp.zeros_like(w)
    return jnp.concatenate(
        [jnp.concatenate([w, z], axis=1), jnp.concatenate([z, w], axis=1)], axis=0
    )


def twice(v):
    return jnp.concatenate([v, v], axis=1)


def norm_weights(w_out, bias, gain):
    w = w_out.astype(F32)
    w = (w - jnp.mean(w, axis=1, keepdims=True)) * gain
    b = (bias - jnp.mean(bias, axis=1, keepdims=True)) * gain
    weights = jnp.transpose(jnp.broadcast_to(1.0 / (LAT * gain * gain), (LAT, LAT)))
    return w.astype(BF16), b, weights.astype(BF16)


def main_kernel(
    counts, nodes, edges_hbm, senders, receivers, stats, halo,
    w_in, w_hid, w_out, e_bias, e_gain, e_shift,
    wn_in, wn_hid, wn_out, n_bias, n_gain, n_shift,
    new_nodes, edges_out,
    edges_v, out_v, zeros_v, ps_t, pr_t, col_t, lr, sidx, ridx,
    w_hid2, w_out2, w_avg2, vecs, acc, work,
    x_ring, or_ring, oh_s, h1_s, h2_s, cg_s, sq_s,
    in_sem, out_sem,
):
    load = pltpu.make_async_copy(edges_hbm, edges_v.at[pl.ds(0, BANDS * SLOTS)], in_sem)
    load.start()
    zeros_v[...] = jnp.zeros_like(zeros_v)

    place = jnp.int32(0)
    for b in range(BANDS):
        count = counts[0, b]
        for j in range(NBLK):
            work[place + NB * STAGES] = jnp.int32(b * NBLK + j)
            place = place + (count > j * BLK).astype(jnp.int32)
    for k in range(NB * STAGES):
        work[k] = jnp.int32(TRASH)
    for k in range(NB * (STAGES + 2) - NB * STAGES + NB * STAGES):
        work[place + NB * STAGES + k] = jnp.int32(TRASH)

    w_snd, w_rcv = w_in[LAT : 2 * LAT], w_in[2 * LAT :]
    w_both = jnp.concatenate([w_snd, w_rcv], axis=1)
    bias1 = e_bias[0:1]
    for k in range(ROWS * COLS // BLK):
        p = dot(nodes[k * BLK : (k + 1) * BLK], w_both)
        ps_t[COLS + k * BLK : COLS + (k + 1) * BLK] = p[:, :LAT].astype(BF16)
        pr_t[k * BLK : (k + 1) * BLK] = (p[:, LAT:] + bias1).astype(BF16)
    p = dot(halo[...], w_snd)
    ps_t[0:COLS] = p[0:32].astype(BF16)
    ps_t[COLS + ROWS * COLS : 2 * COLS + ROWS * COLS] = p[32:64].astype(BF16)
    lr[0, 64:72] = jnp.zeros((8, LAT), F32)
    lr[1, 64:72] = jnp.zeros((8, LAT), F32)
    lr[0, 1:65] = p[64:128]
    lr[1, 1:65] = p[128:192]
    lr[0, 0:1] = p[207:208]
    lr[1, 0:1] = p[223:224]
    lr[0, 65:66] = p[224:225]
    lr[1, 65:66] = p[240:241]
    for b in range(BANDS):
        pair = jnp.concatenate([lr[0, 4 * b : 4 * b + 8], lr[1, 4 * b : 4 * b + 8]], axis=0)
        col_t[16 * b : 16 * b + 16] = pair.astype(BF16)
    pr_t[ROWS * COLS :] = jnp.zeros((BAND_NODES, LAT), BF16)
    ps_t[2 * COLS + ROWS * COLS :] = jnp.zeros((128, LAT), BF16)
    col_t[16 * BANDS :] = jnp.zeros((16, LAT), BF16)

    s = senders[...]
    r = lax.shift_right_logical(s * 241, 13)
    c = s - r * 34
    place_s = jnp.where(c == 0, 192 + r, jnp.where(c == 33, 200 + r, r * 32 + c - 1)).astype(F32)
    place_r = receivers[...].astype(F32)
    for j in range(NBLK):
        sidx[j, 0:BANDS] = place_s[:, j * BLK : (j + 1) * BLK]
        ridx[j, 0:BANDS] = place_r[:, j * BLK : (j + 1) * BLK]

    w_hid2[...] = block_diagonal(w_hid[...])
    w, b3, avg = norm_weights(w_out[...], e_bias[2:3], e_gain[...])
    w_out2[...] = block_diagonal(w)
    w_avg2[...] = block_diagonal(avg)
    vecs[0:1] = twice(e_bias[1:2])
    vecs[1:2] = twice(b3)
    vecs[2:3] = twice(e_shift[...])
    acc[...] = jnp.zeros_like(acc)

    for b in range(BANDS):
        for j in range(2, NBLK):

            @pl.when(counts[0, b] <= j * BLK)
            def _():
                pltpu.make_async_copy(
                    zeros_v, edges_out.at[pl.ds(b * SLOTS + j * BLK, BLK)], out_sem
                ).start()

    load.wait()

    mean, inv = stats[0:1], stats[1:2]
    node_id = lax.broadcasted_iota(jnp.int32, (256, BLK), 0).astype(F32).astype(BF16)
    one, nought = jnp.ones((), BF16), jnp.zeros((), BF16)

    def item(i, stage, u):
        return work[(i + STAGES - stage) * NB + u]

    def step(i, _):
        for u in range(NB):
            k = item(i, 5, u)
            band = lax.shift_right_logical(k, 2)
            slot = lax.rem(i + RING - 5, RING)
            fresh = out_v[pl.ds(pl.multiple_of(k * BLK, BLK), BLK), :]
            acc[band] += dot(or_ring[slot, u], fresh)
        for u in range(NB):
            k = item(i, 4, u)
            band, j = lax.shift_right_logical(k, 2), lax.rem(k, NBLK)
            slot = lax.rem(i + RING - 4, RING)
            var = dot(sq_s[u], w_avg2[...])
            normed = x_ring[slot, u]
            scaled = cg_s[u] * lax.rsqrt(var + EPS) + vecs[2:3]
            left_count = counts[0, jnp.minimum(band, BANDS - 1)] - j * BLK
            slot_id = lax.broadcasted_iota(jnp.int32, (HALF, LAT), 0)
            for h in range(2):
                v = scaled[:, h * LAT : (h + 1) * LAT] + normed[h * HALF : (h + 1) * HALF].astype(F32)
                v = jnp.where(slot_id < left_count - h * HALF, v, 0.0)
                out_v[pl.ds(pl.multiple_of(k * BLK + h * HALF, HALF), HALF), :] = v.astype(BF16)
        for u in range(NB):
            cg = dot(h2_s[u], w_out2[...]) + vecs[1:2]
            cg_s[u] = cg
            sq_s[u] = (cg * cg).astype(BF16)
        for u in range(NB):
            h2_s[u] = jnp.maximum(dot(h1_s[u], w_hid2[...]) + vecs[0:1], 0.0).astype(BF16)
        for u in range(NB):
            k = item(i, 1, u)
            band = lax.shift_right_logical(k, 2)
            slot = lax.rem(i + RING - 1, RING)
            lhs = jnp.concatenate([x_ring[slot, u], oh_s[u]], axis=1)
            start = pl.multiple_of(band * BAND_NODES, BAND_NODES)
            table = jnp.concatenate(
                [
                    w_in[0:LAT],
                    pr_t[pl.ds(start, BAND_NODES), :],
                    ps_t[pl.ds(start, 192), :],
                    col_t[pl.ds(pl.multiple_of(band * 16, 16), 16), :],
                    jnp.zeros((48, LAT), BF16),
                ],
                axis=0,
            )
            h = jnp.maximum(dot(lhs, table), 0.0).astype(BF16)
            h1_s[u] = jnp.concatenate([h[:HALF], h[HALF:]], axis=1)
        for u in range(NB):
            k = item(i, 0, u)
            band, j = lax.shift_right_logical(k, 2), lax.rem(k, NBLK)
            slot = lax.rem(i, RING)
            x = edges_v[pl.ds(pl.multiple_of(k * BLK, BLK), BLK), :].astype(F32)
            x_ring[slot, u] = ((x - mean) * inv).astype(BF16)
            si = sidx[j, pl.ds(band, 1), :].astype(BF16)
            ri = ridx[j, pl.ds(band, 1), :].astype(BF16)
            pick_s = jnp.where(node_id == si, one, nought)
            pick_r = jnp.where(node_id[:BAND_NODES] == ri, one, nought)
            or_ring[slot, u] = pick_r
            oh_s[u, :, 0:LAT] = pick_r.T
            oh_s[u, :, LAT:] = pick_s.T

        @pl.when(i >= 4)
        def _():
            for u in range(NB):
                k = item(i, 4, u)

                @pl.when(k < TRASH)
                def _():
                    pltpu.make_async_copy(
                        out_v.at[pl.ds(pl.multiple_of(k * BLK, BLK), BLK)],
                        edges_out.at[pl.ds(pl.multiple_of(k * BLK, BLK), BLK)],
                        out_sem,
                    ).start()

        return 0

    lax.fori_loop(0, lax.div(place + (NB - 1), NB) + STAGES, step, 0)

    w, b3, avg = norm_weights(wn_out[...], n_bias[2:3], n_gain[...])
    wh2, wo2, wa2 = block_diagonal(wn_hid[...]), block_diagonal(w), block_diagonal(avg)
    bias2, bias3, shift = twice(n_bias[1:2]), twice(b3), twice(n_shift[...])
    size = 2 * BLK
    for k in range(ROWS * COLS // size):
        own = nodes[k * size : (k + 1) * size]
        gathered = jnp.concatenate([acc[k * 4 + t] for t in range(4)], axis=0).astype(BF16)
        h = dot(jnp.concatenate([own, gathered], axis=1), wn_in[...]) + n_bias[0:1]
        h = jnp.maximum(h, 0.0).astype(BF16)
        h = jnp.concatenate([h[:BLK], h[BLK:]], axis=1)
        h = jnp.maximum(dot(h, wh2) + bias2, 0.0).astype(BF16)
        cg = dot(h, wo2) + bias3
        var = dot((cg * cg).astype(BF16), wa2)
        v = cg * lax.rsqrt(var + EPS) + shift
        new_nodes[k * size : k * size + BLK] = (v[:, :LAT] + own[:BLK].astype(F32)).astype(BF16)
        new_nodes[k * size + BLK : (k + 1) * size] = (v[:, LAT:] + own[BLK:].astype(F32)).astype(BF16)
    pltpu.make_async_copy(out_v.at[pl.ds(0, BANDS * SLOTS)], edges_out, out_sem).wait()


def process(counts, nodes, edges, senders, receivers, stats, halo, *params):
    vmem, smem = pl.BlockSpec(memory_space=pltpu.VMEM), pl.BlockSpec(memory_space=pltpu.SMEM)
    any_spec = pl.BlockSpec(memory_space=pl.ANY)
    return pl.pallas_call(
        main_kernel,
        out_shape=(
            jax.ShapeDtypeStruct((ROWS * COLS, LAT), BF16),
            jax.ShapeDtypeStruct((BANDS * SLOTS, LAT), BF16),
        ),
        in_specs=[smem, vmem, any_spec] + [vmem] * (4 + len(params)),
        out_specs=(vmem, any_spec),
        scratch_shapes=[
            pltpu.VMEM(((TRASH + 1) * BLK, LAT), BF16),
            pltpu.VMEM(((TRASH + 1) * BLK, LAT), BF16),
            pltpu.VMEM((BLK, LAT), BF16),
            pltpu.VMEM((ROWS * COLS + 2 * COLS + 128, LAT), BF16),
            pltpu.VMEM((ROWS * COLS + BAND_NODES, LAT), BF16),
            pltpu.VMEM((16 * (BANDS + 1), LAT), BF16),
            pltpu.VMEM((2, 72, LAT), F32),
            pltpu.VMEM((NBLK, 24, BLK), F32),
            pltpu.VMEM((NBLK, 24, BLK), F32),
            pltpu.VMEM((256, 256), BF16),
            pltpu.VMEM((256, 256), BF16),
            pltpu.VMEM((256, 256), BF16),
            pltpu.VMEM((8, 256), F32),
            pltpu.VMEM((BANDS + 1, BAND_NODES, LAT), F32),
            pltpu.SMEM((WORK + NB * STAGES + 8,), jnp.int32),
            pltpu.VMEM((RING, NB, BLK, LAT), BF16),
            pltpu.VMEM((RING, NB, BAND_NODES, BLK), BF16),
            pltpu.VMEM((NB, BLK, 384), BF16),
            pltpu.VMEM((NB, HALF, 256), BF16),
            pltpu.VMEM((NB, HALF, 256), BF16),
            pltpu.VMEM((NB, HALF, 256), F32),
            pltpu.VMEM((NB, HALF, 256), BF16),
            pltpu.SemaphoreType.DMA,
            pltpu.SemaphoreType.DMA,
        ],
        compiler_params=pltpu.CompilerParams(vmem_limit_bytes=50 * 1024 * 1024),
        name="process",
    )(counts, nodes, edges, senders, receivers, stats, halo, *params)


def per_device(
    nodes, edges, senders, receivers, counts,
    w_edge_in, w_edge_hid, w_edge_out, edge_bias, edge_gain, edge_shift,
    w_node_in, w_node_hid, w_node_out, node_bias, node_gain, node_shift,
):
    flat_edges = edges.reshape(BANDS * SLOTS, LAT)
    count_row = counts.reshape(1, BANDS)
    stats, halo = communicate(nodes, flat_edges, count_row)
    new_nodes, new_edges = process(
        count_row, nodes.reshape(ROWS * COLS, LAT), flat_edges,
        senders.reshape(BANDS, SLOTS), receivers.reshape(BANDS, SLOTS), stats, halo,
        w_edge_in, w_edge_hid, w_edge_out, edge_bias, edge_gain.reshape(1, LAT), edge_shift.reshape(1, LAT),
        w_node_in, w_node_hid, w_node_out, node_bias, node_gain.reshape(1, LAT), node_shift.reshape(1, LAT),
    )
    return new_nodes.reshape(nodes.shape), new_edges.reshape(edges.shape)


def solution(mesh):
    in_specs = (
        P("row", "col", None),
        P("row", "col", None, None, None),
        P("row", "col", None, None),
        P("row", "col", None, None),
        P("row", "col", None),
    ) + (P(),) * 12
    out_specs = (P("row", "col", None), P("row", "col", None, None, None))
    return jax.shard_map(
        per_device, mesh=mesh, in_specs=in_specs, out_specs=out_specs, check_vma=False
    )
```

time: 182 us -> 45.8 us (0.25)
  the two profiles are of different devices: /device:TPU:14 before, /device:TPU:1 now
where the time goes in v1:
time: 45.8 us; the launch traced here: 45.5 us
  Pallas kernels  43 us (94%)
  local copies, waits for them, and re-layouts  1.57 us (3%)
  between operations  0.91 us (2%)
    pallas_call x1, Pallas kernels, process(): pl.pallas_call(main_kernel, out_shape=(jax.ShapeDtypeStruct((ROWS * COLS,...  22.5 us
    pallas_call x1, Pallas kernels, communicate(): pl.pallas_call(comm_kernel, out_shape=(jax.ShapeDtypeStruct((8, LAT), F32...  20.6 us
    unnamed x36, local copies, waits for them, and re-layouts  1.57 us

profile of v1, /device:TPU:1, one launch (start us, length us, event | category | flops | bytes accessed | tf_op | source)
XLA Modules:
  0.0 45.5 jit_solution(1685336344235554003)
XLA Ops:
  0.6 0.0 copy-start
  0.6 0.0 copy-start.17
  0.7 0.0 copy-start.16
  0.7 0.0 copy-start.12
  0.7 0.0 copy-start.9
  0.7 0.0 copy-start.8
  0.7 0.0 copy-start.4
  0.7 0.0 copy-start.15
  0.7 0.0 copy-start.14
  0.7 0.0 copy-start.11
  0.7 0.0 copy-start.7
  0.7 0.0 copy-start.6
  0.8 0.0 copy-start.1
  0.8 0.0 copy-start.13
  0.8 0.0 copy-start.3
  0.8 0.0 copy-start.2
  0.8 20.6 %exchange.1 = (f32[8,128]{1,0:T(8,128)}, bf16[256,128]{1,0:T(8,128)(2,1)}) custom-call(bf16[64,32,128]{2,1,0:T(8,128)(2,1)} %nodes_hbm.1, bf16[16384,128]{1,0:T(8,128)(2,1)} %bitcast.20, s32[1,16]{1,0:T(1,128)} %bitcast.14), custom_call_target="tpu_custom_call" | custom-call | tf_op jit(solution)/shard_map/exchange/pallas_call | solution.py:163
  21.4 0.0 copy-done
  21.4 0.0 copy-done.17
  21.4 0.0 copy-done.16
  21.4 0.0 copy-done.12
  21.4 0.0 copy-done.9
  21.4 0.0 copy-done.8
  21.4 0.0 copy-done.4
  21.5 0.0 copy-done.15
  21.5 0.0 copy-done.14
  21.5 0.0 copy-done.11
  21.5 0.0 copy-done.7
  21.5 0.0 copy-done.6
  21.5 0.0 copy-done.1
  21.5 0.0 copy-done.13
  21.5 0.0 copy-done.3
  21.5 0.0 copy-done.2
  21.5 0.0 copy-start.5
  21.6 0.8 %copy-done.5 = bf16[256,128]{1,0:T(8,128)(2,1)S(1)} copy-done((bf16[256,128]{1,0:T(8,128)(2,1)S(1)}, bf16[256,128]{1,0:T(8,128)(2,1)}, u32[]{:S(2)}) %copy-start.5) | copy-done | bytes 65560
  22.4 0.0 copy-start.10
  22.4 0.7 %copy-done.10 = f32[8,128]{1,0:T(8,128)S(1)} copy-done((f32[8,128]{1,0:T(8,128)S(1)}, f32[8,128]{1,0:T(8,128)}, u32[]{:S(2)}) %copy-start.10) | copy-done | bytes 4120
  23.1 22.5 %process.1 = (bf16[2048,128]{1,0:T(8,128)(2,1)}, bf16[16384,128]{1,0:T(8,128)(2,1)}) custom-call(s32[1,16]{1,0:T(1,128)S(1)} %bitcast.15, bf16[2048,128]{1,0:T(8,128)(2,1)S(1)} %bitcast.11, bf16[16384,128]{1,0:T(8,128)(2,1)} %bitcast.21, s32[16,1024]{1,0:T(8,128)S(1)} %bitcast.12, s32[16,1024]{1,0:T(8,128)S(1)} %bitcast.13, f32[8,128]{1,0:T(8,128)S(1)} %copy-done.10, ...), custom_call_target="tpu_custom_call" | custom-call | tf_op jit(solution)/shard_map/process/pallas_call | solution.py:397
Async XLA Ops:
  0.6 20.8 %copy-start = (bf16[64,32,128]{2,1,0:T(8,128)(2,1)S(1)}, bf16[64,32,128]{2,1,0:T(8,128)(2,1)}, u32[]{:S(2)}) copy-start(bf16[64,32,128]{2,1,0:T(8,128)(2,1)} %nodes_hbm.1) | copy-start | bytes 1572868
  0.6 20.8 %copy-start.17 = (f32[128]{0:T(128)S(1)}, f32[128]{0:T(128)}, u32[]{:S(2)}) copy-start(f32[128]{0:T(128)} %param.33) | copy-start | bytes 1540
  0.7 20.8 %copy-start.16 = (f32[128]{0:T(128)S(1)}, f32[128]{0:T(128)}, u32[]{:S(2)}) copy-start(f32[128]{0:T(128)} %param.32) | copy-start | bytes 1540
  0.7 20.8 %copy-start.12 = (f32[3,128]{1,0:T(4,128)S(1)}, f32[3,128]{1,0:T(4,128)}, u32[]{:S(2)}) copy-start(f32[3,128]{1,0:T(4,128)} %n_bias.1) | copy-start | bytes 4612
  0.7 20.8 %copy-start.9 = (bf16[128,128]{1,0:T(8,128)(2,1)S(1)}, bf16[128,128]{1,0:T(8,128)(2,1)}, u32[]{:S(2)}) copy-start(bf16[128,128]{1,0:T(8,128)(2,1)} %wn_out.1) | copy-start | bytes 98308
  0.7 20.8 %copy-start.8 = (bf16[128,128]{1,0:T(8,128)(2,1)S(1)}, bf16[128,128]{1,0:T(8,128)(2,1)}, u32[]{:S(2)}) copy-start(bf16[128,128]{1,0:T(8,128)(2,1)} %wn_hid.1) | copy-start | bytes 98308
  0.7 20.8 %copy-start.4 = (bf16[256,128]{1,0:T(8,128)(2,1)S(1)}, bf16[256,128]{1,0:T(8,128)(2,1)}, u32[]{:S(2)}) copy-start(bf16[256,128]{1,0:T(8,128)(2,1)} %wn_in.1) | copy-start | bytes 196612
  0.7 20.8 %copy-start.15 = (f32[128]{0:T(128)S(1)}, f32[128]{0:T(128)}, u32[]{:S(2)}) copy-start(f32[128]{0:T(128)} %param.27) | copy-start | bytes 1540
  0.7 20.8 %copy-start.14 = (f32[128]{0:T(128)S(1)}, f32[128]{0:T(128)}, u32[]{:S(2)}) copy-start(f32[128]{0:T(128)} %param.26) | copy-start | bytes 1540
  0.7 20.8 %copy-start.11 = (f32[3,128]{1,0:T(4,128)S(1)}, f32[3,128]{1,0:T(4,128)}, u32[]{:S(2)}) copy-start(f32[3,128]{1,0:T(4,128)} %e_bias.1) | copy-start | bytes 4612
  0.7 20.8 %copy-start.7 = (bf16[128,128]{1,0:T(8,128)(2,1)S(1)}, bf16[128,128]{1,0:T(8,128)(2,1)}, u32[]{:S(2)}) copy-start(bf16[128,128]{1,0:T(8,128)(2,1)} %w_out.1) | copy-start | bytes 98308
  0.7 20.8 %copy-start.6 = (bf16[128,128]{1,0:T(8,128)(2,1)S(1)}, bf16[128,128]{1,0:T(8,128)(2,1)}, u32[]{:S(2)}) copy-start(bf16[128,128]{1,0:T(8,128)(2,1)} %w_hid.1) | copy-start | bytes 98308
  0.8 20.8 %copy-start.1 = (bf16[384,128]{1,0:T(8,128)(2,1)S(1)}, bf16[384,128]{1,0:T(8,128)(2,1)}, u32[]{:S(2)}) copy-start(bf16[384,128]{1,0:T(8,128)(2,1)} %w_in.1) | copy-start | bytes 294916
  0.8 20.8 %copy-start.13 = (s32[1,1,16]{2,1,0:T(1,128)S(1)}, s32[1,1,16]{2,1,0:T(1,128)}, u32[]{:S(2)}) copy-start(s32[1,1,16]{2,1,0:T(1,128)} %param.21) | copy-start | bytes 196
  0.8 20.8 %copy-start.3 = (s32[1,1,16,1024]{3,2,1,0:T(8,128)S(1)}, s32[1,1,16,1024]{3,2,1,0:T(8,128)}, u32[]{:S(2)}) copy-start(s32[1,1,16,1024]{3,2,1,0:T(8,128)} %param.20) | copy-start | bytes 196612
  0.8 20.8 %copy-start.2 = (s32[1,1,16,1024]{3,2,1,0:T(8,128)S(1)}, s32[1,1,16,1024]{3,2,1,0:T(8,128)}, u32[]{:S(2)}) copy-start(s32[1,1,16,1024]{3,2,1,0:T(8,128)} %param.19) | copy-start | bytes 196612
  21.5 0.8 %copy-start.5 = (bf16[256,128]{1,0:T(8,128)(2,1)S(1)}, bf16[256,128]{1,0:T(8,128)(2,1)}, u32[]{:S(2)}) copy-start(bf16[256,128]{1,0:T(8,128)(2,1)} %get-tuple-element.7.halo) | copy-start | bytes 196612
  22.4 0.7 %copy-start.10 = (f32[8,128]{1,0:T(8,128)S(1)}, f32[8,128]{1,0:T(8,128)}, u32[]{:S(2)}) copy-start(f32[8,128]{1,0:T(8,128)} %get-tuple-element.6.stats) | copy-start | bytes 12292

commit v2 on v1

v2 whole, which is shorter than its diff:
```python
import functools

import jax
import jax.numpy as jnp
from jax import lax
from jax.experimental import pallas as pl
from jax.experimental.pallas import tpu as pltpu
from jax.sharding import PartitionSpec as P

F32 = jnp.float32
BF16 = jnp.bfloat16
LAT = 128
ROWS = 64
COLS = 32
BANDS = 16
SLOTS = 1024
BAND_NODES = 128
BLK = 256
HALF = BLK // 2
NBLK = SLOTS // BLK
NA = 2
SPLIT = 12
NB = 2
RING = 4
STAGES = 4
TRASH = BANDS * NBLK
EPS = 1e-5
MESH = pl.DeviceIdType.MESH


def combine(parts):
    n = functools.reduce(jnp.add, [p[0:1] for p in parts])
    weighted = functools.reduce(jnp.add, [p[0:1] * p[1:2] for p in parts])
    mean = weighted / n
    m2 = None
    for p in parts:
        d = p[1:2] - mean
        t = p[2:3] + p[0:1] * d * d
        m2 = t if m2 is None else m2 + t
    return n, mean, m2


def dot(a, b):
    return jnp.dot(a, b, preferred_element_type=F32)


def block_diagonal(w):
    z = jnp.zeros_like(w)
    return jnp.concatenate(
        [jnp.concatenate([w, z], axis=1), jnp.concatenate([z, w], axis=1)], axis=0
    )


def twice(v):
    return jnp.concatenate([v, v], axis=1)


def norm_weights(w_out, bias, gain):
    w = w_out.astype(F32)
    w = (w - jnp.mean(w, axis=1, keepdims=True)) * gain
    b = (bias - jnp.mean(bias, axis=1, keepdims=True)) * gain
    weights = jnp.transpose(jnp.broadcast_to(1.0 / (LAT * gain * gain), (LAT, LAT)))
    return w.astype(BF16), b, weights.astype(BF16)


def prepare(hid, out, bias, gain, shift, hid2, out2, avg2, vecs):
    hid2[...] = block_diagonal(hid[...])
    w, b3, avg = norm_weights(out[...], bias[2:3], gain[...])
    out2[...] = block_diagonal(w)
    avg2[...] = block_diagonal(avg)
    vecs[0:1] = twice(bias[1:2])
    vecs[1:2] = twice(b3)
    vecs[2:3] = twice(shift[...])
    vecs[3:4] = twice(bias[0:1])


N_SMALL = 14


def exchange_kernel(*refs):
    nodes_hbm, edges_hbm, counts = refs[:3]
    small_hbm = refs[3 : 3 + N_SMALL]
    (
        stats_out, edges_v, part_v, nodes_v, ridx, w_x2, w_hid2, w_out2, w_avg2, vecs,
        wn_first, wn_hid2, wn_out2, wn_avg2, n_vecs,
    ) = refs[3 + N_SMALL : 18 + N_SMALL]
    small = refs[18 + N_SMALL : 18 + 2 * N_SMALL]
    (
        cols_v, halo_v, mine1, mine2, got1, got2, ps_t, pr_t, col_t, lr, sidx, oh_s,
        edge_sem, node_sem, small_sem, hs_sem, hr_sem, s1_sem, r1_sem, s2_sem, r2_sem,
    ) = refs[18 + 2 * N_SMALL :]
    (
        senders, receivers, w_in, w_hid, w_out, e_bias, e_gain, e_shift,
        wn_in, wn_hid, wn_out, n_bias, n_gain, n_shift,
    ) = small
    n_row, n_col = lax.axis_size("row"), lax.axis_size("col")
    row, col = lax.axis_index("row"), lax.axis_index("col")
    up, down = lax.rem(row + n_row - 1, n_row), lax.rem(row + 1, n_row)
    left, right = lax.rem(col + n_col - 1, n_col), lax.rem(col + 1, n_col)

    barrier = pltpu.get_barrier_semaphore()
    peers = [(row, lax.rem(col + k, n_col)) for k in range(1, n_col)]
    peers += [(lax.rem(row + k, n_row), col) for k in range(1, n_row)]
    peers += [(up, left), (up, right), (down, left), (down, right)]
    for p in peers:
        pl.semaphore_signal(barrier, inc=1, device_id=p, device_id_type=MESH)

    def edge_copy(b):
        return pltpu.make_async_copy(
            edges_hbm.at[pl.ds(b * SLOTS, SLOTS)], edges_v.at[pl.ds(b * SLOTS, SLOTS)], edge_sem.at[b]
        )

    node_copy = pltpu.make_async_copy(nodes_hbm, nodes_v, node_sem)
    for b in range(4):
        edge_copy(b).start()
    node_copy.start()
    for b in range(4, BANDS):
        edge_copy(b).start()
    small_copies = [
        pltpu.make_async_copy(src, dst, small_sem.at[k])
        for k, (src, dst) in enumerate(zip(small_hbm, small))
    ]
    for c in small_copies:
        c.start()

    edge_copy(0).wait()
    pivot = edges_v[0:16, :].astype(F32)[0:1]
    slot_id = lax.broadcasted_iota(jnp.int32, (64, LAT), 0)

    def band_sums(b, s, q):
        count = counts[0, b]
        for j in range(SLOTS // 64):
            d = edges_v[pl.ds(pl.multiple_of(b * SLOTS + j * 64, 64), 64), :].astype(F32) - pivot
            if j >= SLOTS // 128:
                d = jnp.where(slot_id < count - j * 64, d, 0.0)
            e = d * d
            s = s + ((d[0:8] + d[8:16]) + (d[16:24] + d[24:32])) + ((d[32:40] + d[40:48]) + (d[48:56] + d[56:64]))
            q = q + ((e[0:8] + e[8:16]) + (e[16:24] + e[24:32])) + ((e[32:40] + e[40:48]) + (e[48:56] + e[56:64]))
        return s, q

    def band_stats(b, carry):
        edge_copy(b).wait()
        return band_sums(b, *carry)

    zero = jnp.zeros((8, LAT), F32)
    carry = band_sums(0, zero, zero)
    carry = lax.fori_loop(1, 8, band_stats, carry)

    node_copy.wait()
    cols_v[0] = nodes_v[:, 0, :]
    cols_v[1] = nodes_v[:, COLS - 1, :]
    pl.semaphore_wait(barrier, len(peers))

    sends = [
        (nodes_v.at[ROWS - 1], (0, 32), (down, col)),
        (nodes_v.at[0], (32, 32), (up, col)),
        (cols_v.at[1], (64, 64), (row, right)),
        (cols_v.at[0], (128, 64), (row, left)),
        (cols_v.at[1, pl.ds(48, 16)], (192, 16), (down, right)),
        (cols_v.at[0, pl.ds(48, 16)], (208, 16), (down, left)),
        (cols_v.at[1, pl.ds(0, 16)], (224, 16), (up, right)),
        (cols_v.at[0, pl.ds(0, 16)], (240, 16), (up, left)),
    ]
    halo_copies = []
    for k, (src, (start, size), dev) in enumerate(sends):
        c = pltpu.make_async_remote_copy(
            src_ref=src, dst_ref=halo_v.at[pl.ds(start, size)],
            send_sem=hs_sem.at[k], recv_sem=hr_sem.at[k], device_id=dev, device_id_type=MESH,
        )
        c.start()
        halo_copies.append(c)

    s, q = lax.fori_loop(8, BANDS, band_stats, carry)
    total = counts[0, 0]
    for b in range(1, BANDS):
        total = total + counts[0, b]
    n = jnp.full((1, LAT), total.astype(F32))
    s = jnp.sum(s, axis=0, keepdims=True)
    q = jnp.sum(q, axis=0, keepdims=True)
    local_mean = s / n
    filler = jnp.zeros((5, LAT), F32)
    mine1[...] = jnp.concatenate([n, pivot + local_mean, q - s * local_mean, filler], axis=0)

    copies = []
    for k in range(1, n_col):
        c = pltpu.make_async_remote_copy(
            src_ref=mine1, dst_ref=got1.at[k], send_sem=s1_sem.at[k], recv_sem=r1_sem.at[k],
            device_id=(row, lax.rem(col + k, n_col)), device_id_type=MESH,
        )
        c.start()
        copies.append(c)

    for c in small_copies:
        c.wait()
    w_snd, w_rcv = w_in[LAT : 2 * LAT], w_in[2 * LAT :]
    w_both = jnp.concatenate([w_snd, w_rcv], axis=1)
    bias1 = e_bias[0:1]
    for k in range(ROWS * COLS // BLK):
        own = nodes_v[k * 8 : (k + 1) * 8].reshape(BLK, LAT)
        p = dot(own, w_both)
        ps_t[COLS + k * BLK : COLS + (k + 1) * BLK] = p[:, :LAT].astype(BF16)
        pr_t[k * BLK : (k + 1) * BLK] = (p[:, LAT:] + bias1).astype(BF16)

    s = senders[...]
    r = lax.shift_right_logical(s * 241, 13)
    c = s - r * 34
    place_s = jnp.where(c == 0, 192 + r, jnp.where(c == 33, 200 + r, r * 32 + c - 1)).astype(F32)
    place_r = receivers[...].astype(F32)
    for j in range(NBLK):
        sidx[j, 0:BANDS] = place_s[:, j * BLK : (j + 1) * BLK]
        ridx[j, 0:BANDS] = place_r[:, j * BLK : (j + 1) * BLK]

    w_x2[...] = block_diagonal(w_in[0:LAT])
    prepare(w_hid, w_out, e_bias, e_gain, e_shift, w_hid2, w_out2, w_avg2, vecs)

    node_id = lax.broadcasted_iota(jnp.int32, (256, BLK), 0).astype(F32).astype(BF16)
    one, nought = jnp.ones((), BF16), jnp.zeros((), BF16)

    def one_hot(i):
        for u in range(NA):
            k = i * NA + u
            band, j = lax.div(k, NBLK), lax.rem(k, NBLK)
            si = sidx[j, pl.ds(band, 1), :].astype(BF16)
            ri = ridx[j, pl.ds(band, 1), :].astype(BF16)
            pick_s = jnp.where(node_id == si, one, nought)
            pick_r = jnp.where(node_id[:BAND_NODES] == ri, one, nought)
            oh_s[u, :, 0:LAT] = pick_r.T
            oh_s[u, :, LAT:] = pick_s.T

    def gather(i):
        for u in range(NA):
            k = i * NA + u
            band = lax.div(k, NBLK)
            start = pl.multiple_of(band * BAND_NODES, BAND_NODES)
            table = jnp.concatenate(
                [
                    pr_t[pl.ds(start, BAND_NODES), :],
                    ps_t[pl.ds(start, 192), :],
                    col_t[pl.ds(pl.multiple_of(band * 16, 16), 16), :],
                    jnp.zeros((48, LAT), BF16),
                ],
                axis=0,
            )
            part_v[pl.ds(pl.multiple_of(k * BLK, BLK), BLK), :] = dot(oh_s[u], table)

    one_hot(0)
    for c in halo_copies:
        c.wait_recv()
    p = dot(halo_v[...], w_snd)
    ps_t[0:COLS] = p[0:32].astype(BF16)
    ps_t[COLS + ROWS * COLS :] = p[32:64].astype(BF16)
    lr[0, 64:72] = jnp.zeros((8, LAT), F32)
    lr[1, 64:72] = jnp.zeros((8, LAT), F32)
    lr[0, 1:65] = p[64:128]
    lr[1, 1:65] = p[128:192]
    lr[0, 0:1] = p[207:208]
    lr[1, 0:1] = p[223:224]
    lr[0, 65:66] = p[224:225]
    lr[1, 65:66] = p[240:241]
    for b in range(BANDS):
        pair = jnp.concatenate([lr[0, 4 * b : 4 * b + 8], lr[1, 4 * b : 4 * b + 8]], axis=0)
        col_t[16 * b : 16 * b + 16] = pair.astype(BF16)

    last = TRASH // NA - 1

    def step(i, _):
        gather(i)
        one_hot(jnp.minimum(i + 1, last))
        return 0

    lax.fori_loop(0, SPLIT, step, 0)
    for c in copies:
        c.wait_recv()
    n, mean, m2 = combine([mine1[...]] + [got1[k] for k in range(1, n_col)])
    mine2[...] = jnp.concatenate([n, mean, m2, filler], axis=0)
    copies2 = []
    for k in range(1, n_row):
        c = pltpu.make_async_remote_copy(
            src_ref=mine2, dst_ref=got2.at[k], send_sem=s2_sem.at[k], recv_sem=r2_sem.at[k],
            device_id=(lax.rem(row + k, n_row), col), device_id_type=MESH,
        )
        c.start()
        copies2.append(c)
    wn_first[...] = wn_in[...]
    prepare(wn_hid, wn_out, n_bias, n_gain, n_shift, wn_hid2, wn_out2, wn_avg2, n_vecs)
    lax.fori_loop(SPLIT, last + 1, step, 0)
    for c in copies2:
        c.wait_recv()
    n, mean, m2 = combine([mine2[...]] + [got2[k] for k in range(1, n_row)])
    inv = lax.rsqrt(m2 / n + EPS)
    stats_out[...] = jnp.concatenate([mean, inv, jnp.zeros((6, LAT), F32)], axis=0)
    for c in halo_copies + copies + copies2:
        c.wait_send()


def exchange(nodes, edges, counts, *small):
    n_row, n_col = lax.axis_size("row"), lax.axis_size("col")
    hbm, vmem = pl.BlockSpec(memory_space=pltpu.HBM), pl.BlockSpec(memory_space=pltpu.VMEM)
    pin = lambda a: pltpu.with_memory_space_constraint(a, pltpu.HBM)
    square = pltpu.VMEM((256, 256), BF16)
    outs = (
        pltpu.VMEM((8, LAT), F32),
        pltpu.VMEM(((TRASH + 1) * BLK, LAT), BF16),
        pltpu.VMEM(((TRASH + 1) * BLK, LAT), F32),
        pltpu.VMEM((ROWS, COLS, LAT), BF16),
        pltpu.VMEM((NBLK, 24, BLK), F32),
        square, square, square, square, pltpu.VMEM((8, 256), F32),
        pltpu.VMEM((2 * LAT, LAT), BF16), square, square, square, pltpu.VMEM((8, 256), F32),
    )
    return pl.pallas_call(
        exchange_kernel,
        out_shape=outs,
        in_specs=[hbm, hbm, pl.BlockSpec(memory_space=pltpu.SMEM)] + [hbm] * N_SMALL,
        out_specs=(vmem,) * len(outs),
        scratch_shapes=[pltpu.VMEM(a.shape, a.dtype) for a in small]
        + [
            pltpu.VMEM((2, ROWS, LAT), BF16),
            pltpu.VMEM((256, LAT), BF16),
            pltpu.VMEM((8, LAT), F32),
            pltpu.VMEM((8, LAT), F32),
            pltpu.VMEM((n_col, 8, LAT), F32),
            pltpu.VMEM((n_row, 8, LAT), F32),
            pltpu.VMEM((ROWS * COLS + 2 * COLS, LAT), BF16),
            pltpu.VMEM((ROWS * COLS, LAT), BF16),
            pltpu.VMEM((16 * BANDS, LAT), BF16),
            pltpu.VMEM((2, 72, LAT), F32),
            pltpu.VMEM((NBLK, 24, BLK), F32),
            pltpu.VMEM((NA, BLK, 384), BF16),
            pltpu.SemaphoreType.DMA((BANDS,)),
            pltpu.SemaphoreType.DMA,
            pltpu.SemaphoreType.DMA((N_SMALL,)),
            pltpu.SemaphoreType.DMA((8,)),
            pltpu.SemaphoreType.DMA((8,)),
            pltpu.SemaphoreType.DMA((n_col,)),
            pltpu.SemaphoreType.DMA((n_col,)),
            pltpu.SemaphoreType.DMA((n_row,)),
            pltpu.SemaphoreType.DMA((n_row,)),
        ],
        compiler_params=pltpu.CompilerParams(
            collective_id=0, has_side_effects=True, vmem_limit_bytes=32 * 1024 * 1024
        ),
        name="exchange",
    )(pin(nodes), pin(edges), counts, *[pin(a) for a in small])


def main_kernel(
    counts, stats, edges_v, part_v, nodes, ridx, w_x2, w_hid2, w_out2, w_avg2, vecs,
    wn_in, wn_hid2, wn_out2, wn_avg2, n_vecs,
    new_nodes, edges_out,
    out_v, zeros_v, acc, work, x_ring, h1_s, h2_s, cg_s, sq_s, out_sem,
):
    zeros_v[...] = jnp.zeros_like(zeros_v)

    place = jnp.int32(0)
    for b in range(BANDS):
        count = counts[0, b]
        for j in range(NBLK):
            work[place + NB * STAGES] = jnp.int32(b * NBLK + j)
            place = place + (count > j * BLK).astype(jnp.int32)
    for k in range(NB * STAGES):
        work[k] = jnp.int32(TRASH)
    for k in range(NB * (STAGES + 1)):
        work[place + NB * STAGES + k] = jnp.int32(TRASH)
    acc[...] = jnp.zeros_like(acc)
    for b in range(BANDS):
        for j in range(2, NBLK):

            @pl.when(counts[0, b] <= j * BLK)
            def _():
                pltpu.make_async_copy(
                    zeros_v, edges_out.at[pl.ds(b * SLOTS + j * BLK, BLK)], out_sem
                ).start()

    mean, inv = stats[0:1], stats[1:2]
    node_id = lax.broadcasted_iota(jnp.int32, (BAND_NODES, BLK), 0).astype(F32).astype(BF16)
    one, nought = jnp.ones((), BF16), jnp.zeros((), BF16)

    def item(i, stage, u):
        return work[(i + STAGES - stage) * NB + u]

    def step(i, _):
        for u in range(NB):
            k = item(i, 4, u)
            band, j = lax.shift_right_logical(k, 2), lax.rem(k, NBLK)
            fresh = out_v[pl.ds(pl.multiple_of(k * BLK, BLK), BLK), :]
            ri = ridx[j, pl.ds(band, 1), :].astype(BF16)
            acc[band] += dot(jnp.where(node_id == ri, one, nought), fresh)
        for u in range(NB):
            k = item(i, 3, u)
            band, j = lax.shift_right_logical(k, 2), lax.rem(k, NBLK)
            slot = lax.rem(i + RING - 3, RING)
            var = dot(sq_s[u], w_avg2[...])
            scaled = cg_s[u] * lax.rsqrt(var + EPS) + vecs[2:3] + x_ring[slot, u].astype(F32)
            left_count = counts[0, jnp.minimum(band, BANDS - 1)] - j * BLK
            slot_id = lax.broadcasted_iota(jnp.int32, (HALF, LAT), 0)
            for h in range(2):
                v = jnp.where(slot_id < left_count - h * HALF, scaled[:, h * LAT : (h + 1) * LAT], 0.0)
                out_v[pl.ds(pl.multiple_of(k * BLK + h * HALF, HALF), HALF), :] = v.astype(BF16)
        for u in range(NB):
            cg = dot(h2_s[u], w_out2[...]) + vecs[1:2]
            cg_s[u] = cg
            sq_s[u] = (cg * cg).astype(BF16)
        for u in range(NB):
            h2_s[u] = jnp.maximum(dot(h1_s[u], w_hid2[...]) + vecs[0:1], 0.0).astype(BF16)
        for u in range(NB):
            k = item(i, 0, u)
            halves, parts = [], []
            for h in range(2):
                here = pl.ds(pl.multiple_of(k * BLK + h * HALF, HALF), HALF)
                halves.append(((edges_v[here, :].astype(F32) - mean) * inv).astype(BF16))
                parts.append(part_v[here, :])
            x = jnp.concatenate(halves, axis=1)
            x_ring[lax.rem(i, RING), u] = x
            h1 = dot(x, w_x2[...]) + jnp.concatenate(parts, axis=1)
            h1_s[u] = jnp.maximum(h1, 0.0).astype(BF16)

        @pl.when(i >= 3)
        def _():
            for u in range(NB):
                k = item(i, 3, u)

                @pl.when(k < TRASH)
                def _():
                    pltpu.make_async_copy(
                        out_v.at[pl.ds(pl.multiple_of(k * BLK, BLK), BLK)],
                        edges_out.at[pl.ds(pl.multiple_of(k * BLK, BLK), BLK)],
                        out_sem,
                    ).start()

        return 0

    lax.fori_loop(0, lax.div(place + (NB - 1), NB) + STAGES, step, 0)

    size = 2 * BLK
    for k in range(ROWS * COLS // size):
        own = nodes[k * 16 : (k + 1) * 16].reshape(size, LAT)
        gathered = jnp.concatenate([acc[k * 4 + t] for t in range(4)], axis=0).astype(BF16)
        h = dot(jnp.concatenate([own, gathered], axis=1), wn_in[...]) + n_vecs[3:4, 0:LAT]
        h = jnp.maximum(h, 0.0).astype(BF16)
        h = jnp.concatenate([h[:BLK], h[BLK:]], axis=1)
        h = jnp.maximum(dot(h, wn_hid2[...]) + n_vecs[0:1], 0.0).astype(BF16)
        cg = dot(h, wn_out2[...]) + n_vecs[1:2]
        var = dot((cg * cg).astype(BF16), wn_avg2[...])
        v = cg * lax.rsqrt(var + EPS) + n_vecs[2:3]
        new_nodes[k * size : k * size + BLK] = (v[:, :LAT] + own[:BLK].astype(F32)).astype(BF16)
        new_nodes[k * size + BLK : (k + 1) * size] = (v[:, LAT:] + own[BLK:].astype(F32)).astype(BF16)
    pltpu.make_async_copy(out_v.at[pl.ds(0, BANDS * SLOTS)], edges_out, out_sem).wait()


def process(counts, *held):
    vmem, smem = pl.BlockSpec(memory_space=pltpu.VMEM), pl.BlockSpec(memory_space=pltpu.SMEM)
    pin = lambda a: pltpu.with_memory_space_constraint(a, pltpu.VMEM)
    return pl.pallas_call(
        main_kernel,
        out_shape=(
            jax.ShapeDtypeStruct((ROWS * COLS, LAT), BF16),
            jax.ShapeDtypeStruct((BANDS * SLOTS, LAT), BF16),
        ),
        in_specs=[smem] + [vmem] * len(held),
        out_specs=(vmem, pl.BlockSpec(memory_space=pl.ANY)),
        scratch_shapes=[
            pltpu.VMEM(((TRASH + 1) * BLK, LAT), BF16),
            pltpu.VMEM((BLK, LAT), BF16),
            pltpu.VMEM((BANDS + 1, BAND_NODES, LAT), F32),
            pltpu.SMEM((TRASH + NB * (2 * STAGES + 2),), jnp.int32),
            pltpu.VMEM((RING, NB, HALF, 256), BF16),
            pltpu.VMEM((NB, HALF, 256), BF16),
            pltpu.VMEM((NB, HALF, 256), BF16),
            pltpu.VMEM((NB, HALF, 256), F32),
            pltpu.VMEM((NB, HALF, 256), BF16),
            pltpu.SemaphoreType.DMA,
        ],
        compiler_params=pltpu.CompilerParams(vmem_limit_bytes=32 * 1024 * 1024),
        name="process",
    )(counts, *[pin(a) for a in held])


def per_device(
    nodes, edges, senders, receivers, counts,
    w_edge_in, w_edge_hid, w_edge_out, edge_bias, edge_gain, edge_shift,
    w_node_in, w_node_hid, w_node_out, node_bias, node_gain, node_shift,
):
    flat_edges = edges.reshape(BANDS * SLOTS, LAT)
    count_row = counts.reshape(1, BANDS)
    held = exchange(
        nodes, flat_edges, count_row, senders.reshape(BANDS, SLOTS), receivers.reshape(BANDS, SLOTS),
        w_edge_in, w_edge_hid, w_edge_out, edge_bias, edge_gain.reshape(1, LAT), edge_shift.reshape(1, LAT),
        w_node_in, w_node_hid, w_node_out, node_bias, node_gain.reshape(1, LAT), node_shift.reshape(1, LAT),
    )
    new_nodes, new_edges = process(count_row, *held)
    return new_nodes.reshape(nodes.shape), new_edges.reshape(edges.shape)


def solution(mesh):
    in_specs = (
        P("row", "col", None),
        P("row", "col", None, None, None),
        P("row", "col", None, None),
        P("row", "col", None, None),
        P("row", "col", None),
    ) + (P(),) * 12
    out_specs = (P("row", "col", None), P("row", "col", None, None, None))
    return jax.shard_map(
        per_device, mesh=mesh, in_specs=in_specs, out_specs=out_specs, check_vma=False
    )
```

time: 45.8 us -> 40.1 us (0.88)
  Pallas kernels: 43 us -> 38.3 us
  local copies, waits for them, and re-layouts: 1.57 us -> 0.65 us
    pallas_call x1, Pallas kernels: 22.5 us -> 15 us  [process(): pl.pallas_call(main_kernel, out_shape=(jax.ShapeDtypeStruct((ROWS * COLS,...]
    pallas_call x1, Pallas kernels: 20.6 us -> 23.3 us  [exchange(): pl.pallas_call(exchange_kernel, out_shape=outs, in_specs=[hbm, hbm, pl.Bl...]
    unnamed x36 -> x2, local copies, waits for them, and re-layouts: 1.57 us -> 0.65 us
where the time goes in v2:
time: 40.1 us; the launch traced here: 39.6 us
  Pallas kernels  38.3 us (96%)
  local copies, waits for them, and re-layouts  0.65 us (2%)
  between operations  0.65 us (2%)
    pallas_call x1, Pallas kernels, exchange(): pl.pallas_call(exchange_kernel, out_shape=outs, in_specs=[hbm, hbm, pl.Bl...  23.3 us
    pallas_call x1, Pallas kernels, process(): pl.pallas_call(main_kernel, out_shape=(jax.ShapeDtypeStruct((ROWS * COLS,...  15 us

profile of v2, /device:TPU:1, one launch (start us, length us, event | category | flops | bytes accessed | tf_op | source)
XLA Modules:
  0.0 39.6 jit_solution(4618911639340479275)
XLA Ops:
  0.6 0.0 copy-start
  0.6 0.6 %copy-done = s32[1,1,16]{2,1,0:T(1,128)S(1)} copy-done((s32[1,1,16]{2,1,0:T(1,128)S(1)}, s32[1,1,16]{2,1,0:T(1,128)}, u32[]{:S(2)}) %copy-start) | copy-done | bytes 88
  1.3 23.3 %exchange.1 = (f32[8,128]{1,0:T(8,128)S(1)}, bf16[16640,128]{1,0:T(8,128)(2,1)S(1)}, f32[16640,128]{1,0:T(8,128)S(1)}, bf16[64,32,128]{2,1,0:T(8,128)(2,1)S(1)},...) custom-call(bf16[64,32,128]{2,1,0:T(8,128)(2,1)} %refs_0_.1, ...), custom_call_target="tpu_custom_call" | custom-call | tf_op jit(solution)/shard_map/exchange/pallas_call | solution.py:310
  24.6 15.0 %process.1 = (bf16[2048,128]{1,0:T(8,128)(2,1)}, bf16[16384,128]{1,0:T(8,128)(2,1)}) custom-call(s32[1,16]{1,0:T(1,128)S(1)} %bitcast.11, f32[8,128]{1,0:T(8,128)S(1)} %get-tuple-element.19.stats, bf16[16640,128]{1,0:T(8,128)(2,1)S(1)} %get-tuple-element.20.edges_v, f32[16640,128]{1,0:T(8,128)S(1)} %get-tuple-element.21.part_v, ...), custom_call_target="tpu_custom_call" | custom-call | tf_op jit(solution)/shard_map/process/pallas_call | solution.py:453
Async XLA Ops:
  0.6 0.7 %copy-start = (s32[1,1,16]{2,1,0:T(1,128)S(1)}, s32[1,1,16]{2,1,0:T(1,128)}, u32[]{:S(2)}) copy-start(s32[1,1,16]{2,1,0:T(1,128)} %param.21) | copy-start | bytes 196

commit v3 on v2

--- a/solution.py
+++ b/solution.py
@@ -18,11 +18,11 @@
 BLK = 256
 HALF = BLK // 2
 NBLK = SLOTS // BLK
-NA = 2
-SPLIT = 12
-NB = 2
-RING = 4
-STAGES = 4
+NA = 4
+SPLIT = 8
+NB = 4
+RING = 2
+STAGES = 2
 TRASH = BANDS * NBLK
 EPS = 1e-5
 MESH = pl.DeviceIdType.MESH
@@ -78,7 +78,7 @@
 
 
 def exchange_kernel(*refs):
-    nodes_hbm, edges_hbm, counts = refs[:3]
+    nodes_hbm, edges_hbm, counts_hbm = refs[:3]
     small_hbm = refs[3 : 3 + N_SMALL]
     (
         stats_out, edges_v, part_v, nodes_v, ridx, w_x2, w_hid2, w_out2, w_avg2, vecs,
@@ -86,8 +86,8 @@
     ) = refs[3 + N_SMALL : 18 + N_SMALL]
     small = refs[18 + N_SMALL : 18 + 2 * N_SMALL]
     (
-        cols_v, halo_v, mine1, mine2, got1, got2, ps_t, pr_t, col_t, lr, sidx, oh_s,
-        edge_sem, node_sem, small_sem, hs_sem, hr_sem, s1_sem, r1_sem, s2_sem, r2_sem,
+        cols_v, halo_v, mine1, mine2, got1, got2, ps_t, pr_t, col_t, lr, sidx, oh_s, counts,
+        count_sem, edge_sem, node_sem, small_sem, hs_sem, hr_sem, s1_sem, r1_sem, s2_sem, r2_sem,
     ) = refs[18 + 2 * N_SMALL :]
     (
         senders, receivers, w_in, w_hid, w_out, e_bias, e_gain, e_shift,
@@ -110,12 +110,12 @@
             edges_hbm.at[pl.ds(b * SLOTS, SLOTS)], edges_v.at[pl.ds(b * SLOTS, SLOTS)], edge_sem.at[b]
         )
 
+    count_copy = pltpu.make_async_copy(counts_hbm, counts, count_sem)
+    count_copy.start()
     node_copy = pltpu.make_async_copy(nodes_hbm, nodes_v, node_sem)
-    for b in range(4):
+    for b in range(BANDS):
         edge_copy(b).start()
     node_copy.start()
-    for b in range(4, BANDS):
-        edge_copy(b).start()
     small_copies = [
         pltpu.make_async_copy(src, dst, small_sem.at[k])
         for k, (src, dst) in enumerate(zip(small_hbm, small))
@@ -123,6 +123,7 @@
     for c in small_copies:
         c.start()
 
+    count_copy.wait()
     edge_copy(0).wait()
     pivot = edges_v[0:16, :].astype(F32)[0:1]
     slot_id = lax.broadcasted_iota(jnp.int32, (64, LAT), 0)
@@ -144,12 +145,29 @@
 
     zero = jnp.zeros((8, LAT), F32)
     carry = band_sums(0, zero, zero)
-    carry = lax.fori_loop(1, 8, band_stats, carry)
+    s, q = lax.fori_loop(1, BANDS, band_stats, carry)
+    total = counts[0, 0]
+    for b in range(1, BANDS):
+        total = total + counts[0, b]
+    n = jnp.full((1, LAT), total.astype(F32))
+    s = jnp.sum(s, axis=0, keepdims=True)
+    q = jnp.sum(q, axis=0, keepdims=True)
+    local_mean = s / n
+    filler = jnp.zeros((5, LAT), F32)
+    mine1[...] = jnp.concatenate([n, pivot + local_mean, q - s * local_mean, filler], axis=0)
 
     node_copy.wait()
     cols_v[0] = nodes_v[:, 0, :]
     cols_v[1] = nodes_v[:, COLS - 1, :]
     pl.semaphore_wait(barrier, len(peers))
+    copies = []
+    for k in range(1, n_col):
+        c = pltpu.make_async_remote_copy(
+            src_ref=mine1, dst_ref=got1.at[k], send_sem=s1_sem.at[k], recv_sem=r1_sem.at[k],
+            device_id=(row, lax.rem(col + k, n_col)), device_id_type=MESH,
+        )
+        c.start()
+        copies.append(c)
 
     sends = [
         (nodes_v.at[ROWS - 1], (0, 32), (down, col)),
@@ -170,26 +188,6 @@
         c.start()
         halo_copies.append(c)
 
-    s, q = lax.fori_loop(8, BANDS, band_stats, carry)
-    total = counts[0, 0]
-    for b in range(1, BANDS):
-        total = total + counts[0, b]
-    n = jnp.full((1, LAT), total.astype(F32))
-    s = jnp.sum(s, axis=0, keepdims=True)
-    q = jnp.sum(q, axis=0, keepdims=True)
-    local_mean = s / n
-    filler = jnp.zeros((5, LAT), F32)
-    mine1[...] = jnp.concatenate([n, pivot + local_mean, q - s * local_mean, filler], axis=0)
-
-    copies = []
-    for k in range(1, n_col):
-        c = pltpu.make_async_remote_copy(
-            src_ref=mine1, dst_ref=got1.at[k], send_sem=s1_sem.at[k], recv_sem=r1_sem.at[k],
-            device_id=(row, lax.rem(col + k, n_col)), device_id_type=MESH,
-        )
-        c.start()
-        copies.append(c)
-
     for c in small_copies:
         c.wait()
     w_snd, w_rcv = w_in[LAT : 2 * LAT], w_in[2 * LAT :]
@@ -224,8 +222,8 @@
             ri = ridx[j, pl.ds(band, 1), :].astype(BF16)
             pick_s = jnp.where(node_id == si, one, nought)
             pick_r = jnp.where(node_id[:BAND_NODES] == ri, one, nought)
-            oh_s[u, :, 0:LAT] = pick_r.T
-            oh_s[u, :, LAT:] = pick_s.T
+            oh_s[k, :, 0:LAT] = pick_r.T
+            oh_s[k, :, LAT:] = pick_s.T
 
     def gather(i):
         for u in range(NA):
@@ -241,9 +239,14 @@
                 ],
                 axis=0,
             )
-            part_v[pl.ds(pl.multiple_of(k * BLK, BLK), BLK), :] = dot(oh_s[u], table)
-
-    one_hot(0)
+            part_v[pl.ds(pl.multiple_of(k * BLK, BLK), BLK), :] = dot(oh_s[k], table)
+
+    def one_hot_step(i, _):
+        one_hot(i)
+        return 0
+
+    last = TRASH // NA
+    lax.fori_loop(0, last, one_hot_step, 0)
     for c in halo_copies:
         c.wait_recv()
     p = dot(halo_v[...], w_snd)
@@ -261,11 +264,8 @@
         pair = jnp.concatenate([lr[0, 4 * b : 4 * b + 8], lr[1, 4 * b : 4 * b + 8]], axis=0)
         col_t[16 * b : 16 * b + 16] = pair.astype(BF16)
 
-    last = TRASH // NA - 1
-
     def step(i, _):
         gather(i)
-        one_hot(jnp.minimum(i + 1, last))
         return 0
 
     lax.fori_loop(0, SPLIT, step, 0)
@@ -283,7 +283,7 @@
         copies2.append(c)
     wn_first[...] = wn_in[...]
     prepare(wn_hid, wn_out, n_bias, n_gain, n_shift, wn_hid2, wn_out2, wn_avg2, n_vecs)
-    lax.fori_loop(SPLIT, last + 1, step, 0)
+    lax.fori_loop(SPLIT, last, step, 0)
     for c in copies2:
         c.wait_recv()
     n, mean, m2 = combine([mine2[...]] + [got2[k] for k in range(1, n_row)])
@@ -310,7 +310,7 @@
     return pl.pallas_call(
         exchange_kernel,
         out_shape=outs,
-        in_specs=[hbm, hbm, pl.BlockSpec(memory_space=pltpu.SMEM)] + [hbm] * N_SMALL,
+        in_specs=[hbm] * (3 + N_SMALL),
         out_specs=(vmem,) * len(outs),
         scratch_shapes=[pltpu.VMEM(a.shape, a.dtype) for a in small]
         + [
@@ -325,7 +325,9 @@
             pltpu.VMEM((16 * BANDS, LAT), BF16),
             pltpu.VMEM((2, 72, LAT), F32),
             pltpu.VMEM((NBLK, 24, BLK), F32),
-            pltpu.VMEM((NA, BLK, 384), BF16),
+            pltpu.VMEM((TRASH, BLK, 384), BF16),
+            pltpu.SMEM((1, BANDS), jnp.int32),
+            pltpu.SemaphoreType.DMA,
             pltpu.SemaphoreType.DMA((BANDS,)),
             pltpu.SemaphoreType.DMA,
             pltpu.SemaphoreType.DMA((N_SMALL,)),
@@ -337,17 +339,17 @@
             pltpu.SemaphoreType.DMA((n_row,)),
         ],
         compiler_params=pltpu.CompilerParams(
-            collective_id=0, has_side_effects=True, vmem_limit_bytes=32 * 1024 * 1024
+            collective_id=0, has_side_effects=True, vmem_limit_bytes=24 * 1024 * 1024
         ),
         name="exchange",
-    )(pin(nodes), pin(edges), counts, *[pin(a) for a in small])
+    )(pin(nodes), pin(edges), pin(counts), *[pin(a) for a in small])
 
 
 def main_kernel(
     counts, stats, edges_v, part_v, nodes, ridx, w_x2, w_hid2, w_out2, w_avg2, vecs,
     wn_in, wn_hid2, wn_out2, wn_avg2, n_vecs,
     new_nodes, edges_out,
-    out_v, zeros_v, acc, work, x_ring, h1_s, h2_s, cg_s, sq_s, out_sem,
+    out_v, zeros_v, acc, work, x_ring, h2_s, nodes_s, out_sem, node_sem,
 ):
     zeros_v[...] = jnp.zeros_like(zeros_v)
 
@@ -378,46 +380,52 @@
     def item(i, stage, u):
         return work[(i + STAGES - stage) * NB + u]
 
+    slot_id = lax.broadcasted_iota(jnp.int32, (HALF, LAT), 0).astype(F32).astype(BF16)
+    bias2, shift = vecs[0:1].astype(BF16), vecs[2:3].astype(BF16)
+    us = range(NB)
+
+    def where_of(i, stage):
+        ks = [item(i, stage, u) for u in us]
+        return ks, [lax.shift_right_logical(k, 2) for k in ks], [lax.rem(k, NBLK) for k in ks]
+
+    def half_rows(k, h):
+        return pl.ds(pl.multiple_of(k * BLK + h * HALF, HALF), HALF)
+
     def step(i, _):
-        for u in range(NB):
-            k = item(i, 4, u)
-            band, j = lax.shift_right_logical(k, 2), lax.rem(k, NBLK)
-            fresh = out_v[pl.ds(pl.multiple_of(k * BLK, BLK), BLK), :]
-            ri = ridx[j, pl.ds(band, 1), :].astype(BF16)
-            acc[band] += dot(jnp.where(node_id == ri, one, nought), fresh)
-        for u in range(NB):
-            k = item(i, 3, u)
-            band, j = lax.shift_right_logical(k, 2), lax.rem(k, NBLK)
-            slot = lax.rem(i + RING - 3, RING)
-            var = dot(sq_s[u], w_avg2[...])
-            scaled = cg_s[u] * lax.rsqrt(var + EPS) + vecs[2:3] + x_ring[slot, u].astype(F32)
-            left_count = counts[0, jnp.minimum(band, BANDS - 1)] - j * BLK
-            slot_id = lax.broadcasted_iota(jnp.int32, (HALF, LAT), 0)
+        k2, b2, j2 = where_of(i, 2)
+        k1, b1, j1 = where_of(i, 1)
+        k0, _, _ = where_of(i, 0)
+        old, new = lax.rem(i + RING - 1, RING), lax.rem(i, RING)
+        rows = [ridx[j2[u], pl.ds(b2[u], 1), :].astype(BF16) for u in us]
+        for u in us:
+            pick = jnp.where(node_id == rows[u], one, nought)
+            acc[b2[u]] += dot(pick, out_v[pl.ds(pl.multiple_of(k2[u] * BLK, BLK), BLK), :])
+        cgs = [dot(h2_s[u], w_out2[...]) + vecs[1:2] for u in us]
+        h1s = []
+        for u in us:
+            halves = [((edges_v[half_rows(k0[u], h), :].astype(F32) - mean) * inv).astype(BF16) for h in range(2)]
+            x = jnp.concatenate(halves, axis=1)
+            x_ring[new, u] = x
+            parts = [part_v[half_rows(k0[u], h), :] for h in range(2)]
+            h1 = dot(x, w_x2[...]) + jnp.concatenate(parts, axis=1)
+            h1s.append(jnp.maximum(h1.astype(BF16), nought))
+        lows = [cgs[u].astype(BF16) for u in us]
+        variances = [dot(lows[u] * lows[u], w_avg2[...]) for u in us]
+        for u in us:
+            scaled = (cgs[u] * lax.rsqrt(variances[u] + EPS)).astype(BF16) + (x_ring[old, u] + shift)
+            left_count = counts[0, jnp.minimum(b1[u], BANDS - 1)] - j1[u] * BLK
             for h in range(2):
-                v = jnp.where(slot_id < left_count - h * HALF, scaled[:, h * LAT : (h + 1) * LAT], 0.0)
-                out_v[pl.ds(pl.multiple_of(k * BLK + h * HALF, HALF), HALF), :] = v.astype(BF16)
-        for u in range(NB):
-            cg = dot(h2_s[u], w_out2[...]) + vecs[1:2]
-            cg_s[u] = cg
-            sq_s[u] = (cg * cg).astype(BF16)
-        for u in range(NB):
-            h2_s[u] = jnp.maximum(dot(h1_s[u], w_hid2[...]) + vecs[0:1], 0.0).astype(BF16)
-        for u in range(NB):
-            k = item(i, 0, u)
-            halves, parts = [], []
-            for h in range(2):
-                here = pl.ds(pl.multiple_of(k * BLK + h * HALF, HALF), HALF)
-                halves.append(((edges_v[here, :].astype(F32) - mean) * inv).astype(BF16))
-                parts.append(part_v[here, :])
-            x = jnp.concatenate(halves, axis=1)
-            x_ring[lax.rem(i, RING), u] = x
-            h1 = dot(x, w_x2[...]) + jnp.concatenate(parts, axis=1)
-            h1_s[u] = jnp.maximum(h1, 0.0).astype(BF16)
-
-        @pl.when(i >= 3)
+                bound = jnp.clip(left_count - h * HALF, 0, HALF).astype(F32)
+                bound = jnp.full((HALF, LAT), bound).astype(BF16)
+                v = jnp.where(slot_id < bound, scaled[:, h * LAT : (h + 1) * LAT], nought)
+                out_v[half_rows(k1[u], h), :] = v
+        for u in us:
+            h2_s[u] = jnp.maximum(dot(h1s[u], w_hid2[...]).astype(BF16) + bias2, nought)
+
+        @pl.when(i >= 1)
         def _():
             for u in range(NB):
-                k = item(i, 3, u)
+                k = item(i, 1, u)
 
                 @pl.when(k < TRASH)
                 def _():
@@ -432,18 +440,30 @@
     lax.fori_loop(0, lax.div(place + (NB - 1), NB) + STAGES, step, 0)
 
     size = 2 * BLK
-    for k in range(ROWS * COLS // size):
-        own = nodes[k * 16 : (k + 1) * 16].reshape(size, LAT)
+    chunks = range(ROWS * COLS // size)
+    low_bias2, low_shift = n_vecs[0:1].astype(BF16), n_vecs[2:3].astype(BF16)
+    owns = [nodes[k * 16 : (k + 1) * 16].reshape(size, LAT) for k in chunks]
+    hs = []
+    for k in chunks:
         gathered = jnp.concatenate([acc[k * 4 + t] for t in range(4)], axis=0).astype(BF16)
-        h = dot(jnp.concatenate([own, gathered], axis=1), wn_in[...]) + n_vecs[3:4, 0:LAT]
-        h = jnp.maximum(h, 0.0).astype(BF16)
-        h = jnp.concatenate([h[:BLK], h[BLK:]], axis=1)
-        h = jnp.maximum(dot(h, wn_hid2[...]) + n_vecs[0:1], 0.0).astype(BF16)
-        cg = dot(h, wn_out2[...]) + n_vecs[1:2]
-        var = dot((cg * cg).astype(BF16), wn_avg2[...])
-        v = cg * lax.rsqrt(var + EPS) + n_vecs[2:3]
-        new_nodes[k * size : k * size + BLK] = (v[:, :LAT] + own[:BLK].astype(F32)).astype(BF16)
-        new_nodes[k * size + BLK : (k + 1) * size] = (v[:, LAT:] + own[BLK:].astype(F32)).astype(BF16)
+        h = dot(jnp.concatenate([owns[k], gathered], axis=1), wn_in[...]) + n_vecs[3:4, 0:LAT]
+        h = jnp.maximum(h.astype(BF16), nought)
+        hs.append(jnp.concatenate([h[:BLK], h[BLK:]], axis=1))
+    hs = [jnp.maximum(dot(hs[k], wn_hid2[...]).astype(BF16) + low_bias2, nought) for k in chunks]
+    cgs = [dot(hs[k], wn_out2[...]) + n_vecs[1:2] for k in chunks]
+    lows = [cgs[k].astype(BF16) for k in chunks]
+    variances = [dot(lows[k] * lows[k], wn_avg2[...]) for k in chunks]
+    node_copies = []
+    for k in chunks:
+        v = (cgs[k] * lax.rsqrt(variances[k] + EPS)).astype(BF16) + low_shift
+        nodes_s[k * size : k * size + BLK] = v[:, :LAT] + owns[k][:BLK]
+        nodes_s[k * size + BLK : (k + 1) * size] = v[:, LAT:] + owns[k][BLK:]
+        here = pl.ds(k * size, size)
+        c = pltpu.make_async_copy(nodes_s.at[here], new_nodes.at[here], node_sem.at[k])
+        c.start()
+        node_copies.append(c)
+    for c in node_copies:
+        c.wait()
     pltpu.make_async_copy(out_v.at[pl.ds(0, BANDS * SLOTS)], edges_out, out_sem).wait()
 
 
@@ -457,7 +477,7 @@
             jax.ShapeDtypeStruct((BANDS * SLOTS, LAT), BF16),
         ),
         in_specs=[smem] + [vmem] * len(held),
-        out_specs=(vmem, pl.BlockSpec(memory_space=pl.ANY)),
+        out_specs=(pl.BlockSpec(memory_space=pl.ANY), pl.BlockSpec(memory_space=pl.ANY)),
         scratch_shapes=[
             pltpu.VMEM(((TRASH + 1) * BLK, LAT), BF16),
             pltpu.VMEM((BLK, LAT), BF16),
@@ -465,10 +485,9 @@
             pltpu.SMEM((TRASH + NB * (2 * STAGES + 2),), jnp.int32),
             pltpu.VMEM((RING, NB, HALF, 256), BF16),
             pltpu.VMEM((NB, HALF, 256), BF16),
-            pltpu.VMEM((NB, HALF, 256), BF16),
-            pltpu.VMEM((NB, HALF, 256), F32),
-            pltpu.VMEM((NB, HALF, 256), BF16),
+            pltpu.VMEM((ROWS * COLS, LAT), BF16),
             pltpu.SemaphoreType.DMA,
+            pltpu.SemaphoreType.DMA((4,)),
         ],
         compiler_params=pltpu.CompilerParams(vmem_limit_bytes=32 * 1024 * 1024),
         name="process",

time: 40.1 us -> 34.1 us (0.85); the launches traced: 39.6 us -> 34.2 us
  Pallas kernels: 38.3 us -> 33.6 us
  local copies, waits for them, and re-layouts: 0.65 us -> 0.01 us
    pallas_call x1, Pallas kernels: 15 us -> 11.9 us  [process(): pl.pallas_call(main_kernel, out_shape=(jax.ShapeDtypeStruct((ROWS * COLS,...]
    pallas_call x1, Pallas kernels: 23.3 us -> 21.6 us  [exchange(): pl.pallas_call(exchange_kernel, out_shape=outs, in_specs=[hbm] * (3 + N_S...]
    unnamed x2, local copies, waits for them, and re-layouts: 0.65 us -> 0.01 us
where the time goes in v3:
time: 34.1 us; the launch traced here: 34.2 us
  Pallas kernels  33.6 us (99%)
  between operations  0.66 us (2%)
    pallas_call x1, Pallas kernels, exchange(): pl.pallas_call(exchange_kernel, out_shape=outs, in_specs=[hbm] * (3 + N_S...  21.6 us
    pallas_call x1, Pallas kernels, process(): pl.pallas_call(main_kernel, out_shape=(jax.ShapeDtypeStruct((ROWS * COLS,...  11.9 us

profile of v3, /device:TPU:1, one launch (start us, length us, event | category | flops | bytes accessed | tf_op | source)
XLA Modules:
  0.0 34.2 jit_solution(18251546559751739514)
XLA Ops:
  0.6 0.0 copy-start
  0.6 21.6 %exchange.1 = (f32[8,128]{1,0:T(8,128)S(1)}, bf16[16640,128]{1,0:T(8,128)(2,1)S(1)}, f32[16640,128]{1,0:T(8,128)S(1)}, bf16[64,32,128]{2,1,0:T(8,128)(2,1)S(1)},...) custom-call(bf16[64,32,128]{2,1,0:T(8,128)(2,1)} %refs_0_.1, ...), custom_call_target="tpu_custom_call" | custom-call | tf_op jit(solution)/shard_map/exchange/pallas_call | solution.py:310
  22.3 0.0 copy-done
  22.3 11.9 %process.1 = (bf16[2048,128]{1,0:T(8,128)(2,1)}, bf16[16384,128]{1,0:T(8,128)(2,1)}) custom-call(s32[1,16]{1,0:T(1,128)S(1)} %bitcast.11, f32[8,128]{1,0:T(8,128)S(1)} %get-tuple-element.19.stats, bf16[16640,128]{1,0:T(8,128)(2,1)S(1)} %get-tuple-element.20.edges_v, f32[16640,128]{1,0:T(8,128)S(1)} %get-tuple-element.21.part_v, ...), custom_call_target="tpu_custom_call" | custom-call | tf_op jit(solution)/shard_map/process/pallas_call | solution.py:473
Async XLA Ops:
  0.6 21.7 %copy-start = (s32[1,1,16]{2,1,0:T(1,128)S(1)}, s32[1,1,16]{2,1,0:T(1,128)}, u32[]{:S(2)}) copy-start(s32[1,1,16]{2,1,0:T(1,128)} %param.21) | copy-start | bytes 196

commit v4 on v3

--- a/solution.py
+++ b/solution.py
@@ -18,8 +18,8 @@
 BLK = 256
 HALF = BLK // 2
 NBLK = SLOTS // BLK
-NA = 4
-SPLIT = 8
+NA = 8
+NP = 4
 NB = 4
 RING = 2
 STAGES = 2
@@ -153,7 +153,7 @@
     s = jnp.sum(s, axis=0, keepdims=True)
     q = jnp.sum(q, axis=0, keepdims=True)
     local_mean = s / n
-    filler = jnp.zeros((5, LAT), F32)
+    filler = jnp.zeros((1, LAT), F32)
     mine1[...] = jnp.concatenate([n, pivot + local_mean, q - s * local_mean, filler], axis=0)
 
     node_copy.wait()
@@ -214,61 +214,39 @@
     node_id = lax.broadcasted_iota(jnp.int32, (256, BLK), 0).astype(F32).astype(BF16)
     one, nought = jnp.ones((), BF16), jnp.zeros((), BF16)
 
-    def one_hot(i):
+    ps_t[0:COLS] = jnp.zeros((COLS, LAT), BF16)
+    ps_t[COLS + ROWS * COLS :] = jnp.zeros((COLS, LAT), BF16)
+
+    def one_hot(k):
+        band, j = lax.div(k, NBLK), lax.rem(k, NBLK)
+        si = sidx[j, pl.ds(band, 1), :].astype(BF16)
+        ri = ridx[j, pl.ds(band, 1), :].astype(BF16)
+        pick_s = jnp.where(node_id == si, one, nought)
+        pick_r = jnp.where(node_id[:BAND_NODES] == ri, one, nought)
+        oh_s[k, :, 0:LAT] = pick_r.T
+        oh_s[k, :, LAT:] = pick_s.T
+
+    def gather(k):
+        start = pl.multiple_of(lax.div(k, NBLK) * BAND_NODES, BAND_NODES)
+        table = jnp.concatenate(
+            [pr_t[pl.ds(start, BAND_NODES), :], ps_t[pl.ds(start, 192), :], jnp.zeros((64, LAT), BF16)],
+            axis=0,
+        )
+        part_v[pl.ds(pl.multiple_of(k * BLK, BLK), BLK), :] = dot(oh_s[k], table)
+
+    last = TRASH // NA - 1
+    for u in range(NA):
+        one_hot(jnp.int32(u))
+
+    def step(i, _):
         for u in range(NA):
-            k = i * NA + u
-            band, j = lax.div(k, NBLK), lax.rem(k, NBLK)
-            si = sidx[j, pl.ds(band, 1), :].astype(BF16)
-            ri = ridx[j, pl.ds(band, 1), :].astype(BF16)
-            pick_s = jnp.where(node_id == si, one, nought)
-            pick_r = jnp.where(node_id[:BAND_NODES] == ri, one, nought)
-            oh_s[k, :, 0:LAT] = pick_r.T
-            oh_s[k, :, LAT:] = pick_s.T
-
-    def gather(i):
+            gather(i * NA + u)
         for u in range(NA):
-            k = i * NA + u
-            band = lax.div(k, NBLK)
-            start = pl.multiple_of(band * BAND_NODES, BAND_NODES)
-            table = jnp.concatenate(
-                [
-                    pr_t[pl.ds(start, BAND_NODES), :],
-                    ps_t[pl.ds(start, 192), :],
-                    col_t[pl.ds(pl.multiple_of(band * 16, 16), 16), :],
-                    jnp.zeros((48, LAT), BF16),
-                ],
-                axis=0,
-            )
-            part_v[pl.ds(pl.multiple_of(k * BLK, BLK), BLK), :] = dot(oh_s[k], table)
-
-    def one_hot_step(i, _):
-        one_hot(i)
+            one_hot(jnp.minimum(i + 1, last) * NA + u)
         return 0
 
-    last = TRASH // NA
-    lax.fori_loop(0, last, one_hot_step, 0)
-    for c in halo_copies:
-        c.wait_recv()
-    p = dot(halo_v[...], w_snd)
-    ps_t[0:COLS] = p[0:32].astype(BF16)
-    ps_t[COLS + ROWS * COLS :] = p[32:64].astype(BF16)
-    lr[0, 64:72] = jnp.zeros((8, LAT), F32)
-    lr[1, 64:72] = jnp.zeros((8, LAT), F32)
-    lr[0, 1:65] = p[64:128]
-    lr[1, 1:65] = p[128:192]
-    lr[0, 0:1] = p[207:208]
-    lr[1, 0:1] = p[223:224]
-    lr[0, 65:66] = p[224:225]
-    lr[1, 65:66] = p[240:241]
-    for b in range(BANDS):
-        pair = jnp.concatenate([lr[0, 4 * b : 4 * b + 8], lr[1, 4 * b : 4 * b + 8]], axis=0)
-        col_t[16 * b : 16 * b + 16] = pair.astype(BF16)
-
-    def step(i, _):
-        gather(i)
-        return 0
-
-    lax.fori_loop(0, SPLIT, step, 0)
+    lax.fori_loop(0, last + 1, step, 0)
+
     for c in copies:
         c.wait_recv()
     n, mean, m2 = combine([mine1[...]] + [got1[k] for k in range(1, n_col)])
@@ -281,9 +259,51 @@
         )
         c.start()
         copies2.append(c)
+
+    for c in halo_copies:
+        c.wait_recv()
+    p = dot(halo_v[...], w_snd)
+    lr[0, 64:72] = jnp.zeros((8, LAT), F32)
+    lr[1, 64:72] = jnp.zeros((8, LAT), F32)
+    lr[0, 1:65] = p[64:128]
+    lr[1, 1:65] = p[128:192]
+    lr[0, 0:1] = p[207:208]
+    lr[1, 0:1] = p[223:224]
+    lr[0, 65:66] = p[224:225]
+    lr[1, 65:66] = p[240:241]
+    top = jnp.concatenate([p[0:32].astype(BF16), jnp.zeros((96, LAT), BF16)], axis=0)
+    col_t[:, 0:64] = jnp.zeros((BANDS, 64, LAT), BF16)
+    col_t[BANDS - 1, 32:64] = p[32:64].astype(BF16)
+    col_t[:, 80:] = jnp.zeros((BANDS, 48, LAT), BF16)
+    for b in range(BANDS):
+        pair = jnp.concatenate([lr[0, 4 * b : 4 * b + 8], lr[1, 4 * b : 4 * b + 8]], axis=0)
+        col_t[b, 64:80] = pair.astype(BF16)
+
+    def halo_step(i, _):
+        bands = [i * NP + u for u in range(NP)]
+        tables = [block_diagonal(col_t[b]) for b in bands]
+        lhs = [
+            [jnp.concatenate([oh_s[b * NBLK + j, :HALF, 2 * LAT :], oh_s[b * NBLK + j, HALF:, 2 * LAT :]], axis=1) for j in range(NBLK)]
+            for b in bands
+        ]
+        for u, b in enumerate(bands):
+            more = dot(jnp.concatenate(lhs[u], axis=0), tables[u])
+            for j in range(NBLK):
+                for h in range(2):
+                    here = pl.ds(pl.multiple_of((b * NBLK + j) * BLK + h * HALF, HALF), HALF)
+                    part_v[here, :] += more[j * HALF : (j + 1) * HALF, h * LAT : (h + 1) * LAT]
+        return 0
+
+    lax.fori_loop(0, BANDS // NP, halo_step, 0)
+    tops = block_diagonal(top)
+    lhs = [jnp.concatenate([oh_s[j, :HALF, LAT : 2 * LAT], oh_s[j, HALF:, LAT : 2 * LAT]], axis=1) for j in range(NBLK)]
+    more = dot(jnp.concatenate(lhs, axis=0), tops)
+    for j in range(NBLK):
+        for h in range(2):
+            here = slice(j * BLK + h * HALF, j * BLK + (h + 1) * HALF)
+            part_v[here] += more[j * HALF : (j + 1) * HALF, h * LAT : (h + 1) * LAT]
     wn_first[...] = wn_in[...]
     prepare(wn_hid, wn_out, n_bias, n_gain, n_shift, wn_hid2, wn_out2, wn_avg2, n_vecs)
-    lax.fori_loop(SPLIT, last, step, 0)
     for c in copies2:
         c.wait_recv()
     n, mean, m2 = combine([mine2[...]] + [got2[k] for k in range(1, n_row)])
@@ -316,13 +336,13 @@
         + [
             pltpu.VMEM((2, ROWS, LAT), BF16),
             pltpu.VMEM((256, LAT), BF16),
-            pltpu.VMEM((8, LAT), F32),
-            pltpu.VMEM((8, LAT), F32),
-            pltpu.VMEM((n_col, 8, LAT), F32),
-            pltpu.VMEM((n_row, 8, LAT), F32),
+            pltpu.VMEM((4, LAT), F32),
+            pltpu.VMEM((4, LAT), F32),
+            pltpu.VMEM((n_col, 4, LAT), F32),
+            pltpu.VMEM((n_row, 4, LAT), F32),
             pltpu.VMEM((ROWS * COLS + 2 * COLS, LAT), BF16),
             pltpu.VMEM((ROWS * COLS, LAT), BF16),
-            pltpu.VMEM((16 * BANDS, LAT), BF16),
+            pltpu.VMEM((BANDS, BAND_NODES, LAT), BF16),
             pltpu.VMEM((2, 72, LAT), F32),
             pltpu.VMEM((NBLK, 24, BLK), F32),
             pltpu.VMEM((TRASH, BLK, 384), BF16),
@@ -391,16 +411,20 @@
     def half_rows(k, h):
         return pl.ds(pl.multiple_of(k * BLK + h * HALF, HALF), HALF)
 
-    def step(i, _):
+    def scatter(i):
         k2, b2, j2 = where_of(i, 2)
-        k1, b1, j1 = where_of(i, 1)
-        k0, _, _ = where_of(i, 0)
-        old, new = lax.rem(i + RING - 1, RING), lax.rem(i, RING)
         rows = [ridx[j2[u], pl.ds(b2[u], 1), :].astype(BF16) for u in us]
         for u in us:
             pick = jnp.where(node_id == rows[u], one, nought)
             acc[b2[u]] += dot(pick, out_v[pl.ds(pl.multiple_of(k2[u] * BLK, BLK), BLK), :])
+
+    def output():
         cgs = [dot(h2_s[u], w_out2[...]) + vecs[1:2] for u in us]
+        return cgs
+
+    def first(i):
+        k0, _, _ = where_of(i, 0)
+        new = lax.rem(i, RING)
         h1s = []
         for u in us:
             halves = [((edges_v[half_rows(k0[u], h), :].astype(F32) - mean) * inv).astype(BF16) for h in range(2)]
@@ -409,8 +433,16 @@
             parts = [part_v[half_rows(k0[u], h), :] for h in range(2)]
             h1 = dot(x, w_x2[...]) + jnp.concatenate(parts, axis=1)
             h1s.append(jnp.maximum(h1.astype(BF16), nought))
+        return h1s
+
+    def variance(cgs):
         lows = [cgs[u].astype(BF16) for u in us]
         variances = [dot(lows[u] * lows[u], w_avg2[...]) for u in us]
+        return variances
+
+    def finish(i, cgs, variances):
+        k1, b1, j1 = where_of(i, 1)
+        old = lax.rem(i + RING - 1, RING)
         for u in us:
             scaled = (cgs[u] * lax.rsqrt(variances[u] + EPS)).astype(BF16) + (x_ring[old, u] + shift)
             left_count = counts[0, jnp.minimum(b1[u], BANDS - 1)] - j1[u] * BLK
@@ -419,25 +451,34 @@
                 bound = jnp.full((HALF, LAT), bound).astype(BF16)
                 v = jnp.where(slot_id < bound, scaled[:, h * LAT : (h + 1) * LAT], nought)
                 out_v[half_rows(k1[u], h), :] = v
+
+    def hidden(h1s):
         for u in us:
             h2_s[u] = jnp.maximum(dot(h1s[u], w_hid2[...]).astype(BF16) + bias2, nought)
 
-        @pl.when(i >= 1)
-        def _():
-            for u in range(NB):
-                k = item(i, 1, u)
-
-                @pl.when(k < TRASH)
-                def _():
-                    pltpu.make_async_copy(
-                        out_v.at[pl.ds(pl.multiple_of(k * BLK, BLK), BLK)],
-                        edges_out.at[pl.ds(pl.multiple_of(k * BLK, BLK), BLK)],
-                        out_sem,
-                    ).start()
-
+    def step(i, _):
+        scatter(i)
+        cgs = output()
+        h1s = first(i)
+        variances = variance(cgs)
+        finish(i, cgs, variances)
+        hidden(h1s)
+        for u in range(NB):
+            k = item(i, 1, u)
+
+            @pl.when(k < TRASH)
+            def _():
+                pltpu.make_async_copy(
+                    out_v.at[pl.ds(pl.multiple_of(k * BLK, BLK), BLK)],
+                    edges_out.at[pl.ds(pl.multiple_of(k * BLK, BLK), BLK)],
+                    out_sem,
+                ).start()
         return 0
 
-    lax.fori_loop(0, lax.div(place + (NB - 1), NB) + STAGES, step, 0)
+    steps = lax.div(place + (NB - 1), NB) + 1
+    hidden(first(0))
+    lax.fori_loop(1, steps, step, 0)
+    scatter(steps)
 
     size = 2 * BLK
     chunks = range(ROWS * COLS // size)

time: 34.1 us -> 31.1 us (0.912)
  Pallas kernels: 33.6 us -> 30.5 us
    pallas_call x1, Pallas kernels: 21.6 us -> 19.9 us  [exchange(): pl.pallas_call(exchange_kernel, out_shape=outs, in_specs=[hbm] * (3 + N_S...]
    pallas_call x1, Pallas kernels: 11.9 us -> 10.7 us  [process(): pl.pallas_call(main_kernel, out_shape=(jax.ShapeDtypeStruct((ROWS * COLS,...]
where the time goes in v4:
time: 31.1 us; the launch traced here: 31.2 us
  Pallas kernels  30.5 us (98%)
  between operations  0.66 us (2%)
    pallas_call x1, Pallas kernels, exchange(): pl.pallas_call(exchange_kernel, out_shape=outs, in_specs=[hbm] * (3 + N_S...  19.9 us
    pallas_call x1, Pallas kernels, process(): pl.pallas_call(main_kernel, out_shape=(jax.ShapeDtypeStruct((ROWS * COLS,...  10.7 us

profile of v4, /device:TPU:1, one launch (start us, length us, event | category | flops | bytes accessed | tf_op | source)
XLA Modules:
  0.0 31.2 jit_solution(3236518479124366672)
XLA Ops:
  0.6 0.0 copy-start
  0.6 19.9 %exchange.1 = (f32[8,128]{1,0:T(8,128)S(1)}, bf16[16640,128]{1,0:T(8,128)(2,1)S(1)}, f32[16640,128]{1,0:T(8,128)S(1)}, bf16[64,32,128]{2,1,0:T(8,128)(2,1)S(1)},...) custom-call(bf16[64,32,128]{2,1,0:T(8,128)(2,1)} %refs_0_.1, ...), custom_call_target="tpu_custom_call" | custom-call | tf_op jit(solution)/shard_map/exchange/pallas_call | solution.py:330
  20.5 0.0 copy-done
  20.5 10.7 %process.1 = (bf16[2048,128]{1,0:T(8,128)(2,1)}, bf16[16384,128]{1,0:T(8,128)(2,1)}) custom-call(s32[1,16]{1,0:T(1,128)S(1)} %bitcast.11, f32[8,128]{1,0:T(8,128)S(1)} %get-tuple-element.19.stats, bf16[16640,128]{1,0:T(8,128)(2,1)S(1)} %get-tuple-element.20.edges_v, f32[16640,128]{1,0:T(8,128)S(1)} %get-tuple-element.21.part_v, ...), custom_call_target="tpu_custom_call" | custom-call | tf_op jit(solution)/shard_map/process/pallas_call | solution.py:514
Async XLA Ops:
  0.6 19.9 %copy-start = (s32[1,1,16]{2,1,0:T(1,128)S(1)}, s32[1,1,16]{2,1,0:T(1,128)}, u32[]{:S(2)}) copy-start(s32[1,1,16]{2,1,0:T(1,128)} %param.21) | copy-start | bytes 196

commit v5 on v4

--- a/solution.py
+++ b/solution.py
@@ -19,8 +19,10 @@
 HALF = BLK // 2
 NBLK = SLOTS // BLK
 NA = 8
+SPLIT = 4
 NP = 4
 NB = 4
+GROUP = 2
 RING = 2
 STAGES = 2
 TRASH = BANDS * NBLK
@@ -72,6 +74,7 @@
     vecs[1:2] = twice(b3)
     vecs[2:3] = twice(shift[...])
     vecs[3:4] = twice(bias[0:1])
+    vecs[4:5] = twice(1.0 / (LAT * gain[...] * gain[...]))
 
 
 N_SMALL = 14
@@ -98,22 +101,23 @@
     up, down = lax.rem(row + n_row - 1, n_row), lax.rem(row + 1, n_row)
     left, right = lax.rem(col + n_col - 1, n_col), lax.rem(col + 1, n_col)
 
+    def edge_copy(b):
+        return pltpu.make_async_copy(
+            edges_hbm.at[pl.ds(b * SLOTS, SLOTS)], edges_v.at[pl.ds(b * SLOTS, SLOTS)], edge_sem.at[b]
+        )
+
+    node_copy = pltpu.make_async_copy(nodes_hbm, nodes_v, node_sem)
+    for b in range(2):
+        edge_copy(b).start()
+    count_copy = pltpu.make_async_copy(counts_hbm, counts, count_sem)
+    count_copy.start()
     barrier = pltpu.get_barrier_semaphore()
     peers = [(row, lax.rem(col + k, n_col)) for k in range(1, n_col)]
     peers += [(lax.rem(row + k, n_row), col) for k in range(1, n_row)]
     peers += [(up, left), (up, right), (down, left), (down, right)]
     for p in peers:
         pl.semaphore_signal(barrier, inc=1, device_id=p, device_id_type=MESH)
-
-    def edge_copy(b):
-        return pltpu.make_async_copy(
-            edges_hbm.at[pl.ds(b * SLOTS, SLOTS)], edges_v.at[pl.ds(b * SLOTS, SLOTS)], edge_sem.at[b]
-        )
-
-    count_copy = pltpu.make_async_copy(counts_hbm, counts, count_sem)
-    count_copy.start()
-    node_copy = pltpu.make_async_copy(nodes_hbm, nodes_v, node_sem)
-    for b in range(BANDS):
+    for b in range(2, BANDS):
         edge_copy(b).start()
     node_copy.start()
     small_copies = [
@@ -125,15 +129,18 @@
 
     count_copy.wait()
     edge_copy(0).wait()
-    pivot = edges_v[0:16, :].astype(F32)[0:1]
-    slot_id = lax.broadcasted_iota(jnp.int32, (64, LAT), 0)
+    low_pivot = edges_v[0:16, :][0:1]
+    pivot = low_pivot.astype(F32)
+    slot_id = lax.broadcasted_iota(jnp.int32, (64, LAT), 0).astype(F32).astype(BF16)
 
     def band_sums(b, s, q):
         count = counts[0, b]
         for j in range(SLOTS // 64):
-            d = edges_v[pl.ds(pl.multiple_of(b * SLOTS + j * 64, 64), 64), :].astype(F32) - pivot
+            x = edges_v[pl.ds(pl.multiple_of(b * SLOTS + j * 64, 64), 64), :]
             if j >= SLOTS // 128:
-                d = jnp.where(slot_id < count - j * 64, d, 0.0)
+                bound = jnp.clip(count - j * 64, 0, 64).astype(F32)
+                x = jnp.where(slot_id < jnp.full((64, LAT), bound).astype(BF16), x, low_pivot)
+            d = x.astype(F32) - pivot
             e = d * d
             s = s + ((d[0:8] + d[8:16]) + (d[16:24] + d[24:32])) + ((d[32:40] + d[40:48]) + (d[48:56] + d[56:64]))
             q = q + ((e[0:8] + e[8:16]) + (e[16:24] + e[24:32])) + ((e[32:40] + e[40:48]) + (e[48:56] + e[56:64]))
@@ -161,10 +168,10 @@
     cols_v[1] = nodes_v[:, COLS - 1, :]
     pl.semaphore_wait(barrier, len(peers))
     copies = []
-    for k in range(1, n_col):
+    for k in range(1, n_row):
         c = pltpu.make_async_remote_copy(
             src_ref=mine1, dst_ref=got1.at[k], send_sem=s1_sem.at[k], recv_sem=r1_sem.at[k],
-            device_id=(row, lax.rem(col + k, n_col)), device_id_type=MESH,
+            device_id=(lax.rem(row + k, n_row), col), device_id_type=MESH,
         )
         c.start()
         copies.append(c)
@@ -245,20 +252,20 @@
             one_hot(jnp.minimum(i + 1, last) * NA + u)
         return 0
 
-    lax.fori_loop(0, last + 1, step, 0)
-
+    lax.fori_loop(0, SPLIT, step, 0)
     for c in copies:
         c.wait_recv()
-    n, mean, m2 = combine([mine1[...]] + [got1[k] for k in range(1, n_col)])
+    n, mean, m2 = combine([mine1[...]] + [got1[k] for k in range(1, n_row)])
     mine2[...] = jnp.concatenate([n, mean, m2, filler], axis=0)
     copies2 = []
-    for k in range(1, n_row):
+    for k in range(1, n_col):
         c = pltpu.make_async_remote_copy(
             src_ref=mine2, dst_ref=got2.at[k], send_sem=s2_sem.at[k], recv_sem=r2_sem.at[k],
-            device_id=(lax.rem(row + k, n_row), col), device_id_type=MESH,
+            device_id=(row, lax.rem(col + k, n_col)), device_id_type=MESH,
         )
         c.start()
         copies2.append(c)
+    lax.fori_loop(SPLIT, last + 1, step, 0)
 
     for c in halo_copies:
         c.wait_recv()
@@ -306,7 +313,7 @@
     prepare(wn_hid, wn_out, n_bias, n_gain, n_shift, wn_hid2, wn_out2, wn_avg2, n_vecs)
     for c in copies2:
         c.wait_recv()
-    n, mean, m2 = combine([mine2[...]] + [got2[k] for k in range(1, n_row)])
+    n, mean, m2 = combine([mine2[...]] + [got2[k] for k in range(1, n_col)])
     inv = lax.rsqrt(m2 / n + EPS)
     stats_out[...] = jnp.concatenate([mean, inv, jnp.zeros((6, LAT), F32)], axis=0)
     for c in halo_copies + copies + copies2:
@@ -338,8 +345,8 @@
             pltpu.VMEM((256, LAT), BF16),
             pltpu.VMEM((4, LAT), F32),
             pltpu.VMEM((4, LAT), F32),
+            pltpu.VMEM((n_row, 4, LAT), F32),
             pltpu.VMEM((n_col, 4, LAT), F32),
-            pltpu.VMEM((n_row, 4, LAT), F32),
             pltpu.VMEM((ROWS * COLS + 2 * COLS, LAT), BF16),
             pltpu.VMEM((ROWS * COLS, LAT), BF16),
             pltpu.VMEM((BANDS, BAND_NODES, LAT), BF16),
@@ -353,10 +360,10 @@
             pltpu.SemaphoreType.DMA((N_SMALL,)),
             pltpu.SemaphoreType.DMA((8,)),
             pltpu.SemaphoreType.DMA((8,)),
+            pltpu.SemaphoreType.DMA((n_row,)),
+            pltpu.SemaphoreType.DMA((n_row,)),
             pltpu.SemaphoreType.DMA((n_col,)),
             pltpu.SemaphoreType.DMA((n_col,)),
-            pltpu.SemaphoreType.DMA((n_row,)),
-            pltpu.SemaphoreType.DMA((n_row,)),
         ],
         compiler_params=pltpu.CompilerParams(
             collective_id=0, has_side_effects=True, vmem_limit_bytes=24 * 1024 * 1024
@@ -418,43 +425,63 @@
             pick = jnp.where(node_id == rows[u], one, nought)
             acc[b2[u]] += dot(pick, out_v[pl.ds(pl.multiple_of(k2[u] * BLK, BLK), BLK), :])
 
+    groups = range(NB // GROUP)
+
+    def rows_of(g, t):
+        return slice((g * GROUP + t) * HALF, (g * GROUP + t + 1) * HALF)
+
+    def group(g):
+        return slice(g * GROUP * HALF, (g + 1) * GROUP * HALF)
+
     def output():
-        cgs = [dot(h2_s[u], w_out2[...]) + vecs[1:2] for u in us]
-        return cgs
+        return [dot(h2_s[group(g)], w_out2[...]) + vecs[1:2] for g in groups]
 
     def first(i):
         k0, _, _ = where_of(i, 0)
         new = lax.rem(i, RING)
         h1s = []
-        for u in us:
-            halves = [((edges_v[half_rows(k0[u], h), :].astype(F32) - mean) * inv).astype(BF16) for h in range(2)]
-            x = jnp.concatenate(halves, axis=1)
-            x_ring[new, u] = x
-            parts = [part_v[half_rows(k0[u], h), :] for h in range(2)]
-            h1 = dot(x, w_x2[...]) + jnp.concatenate(parts, axis=1)
+        for g in groups:
+            xs, parts = [], []
+            for t in range(GROUP):
+                k = k0[g * GROUP + t]
+                halves = [((edges_v[half_rows(k, h), :].astype(F32) - mean) * inv).astype(BF16) for h in range(2)]
+                xs.append(jnp.concatenate(halves, axis=1))
+                parts.append(jnp.concatenate([part_v[half_rows(k, h), :] for h in range(2)], axis=1))
+            x = jnp.concatenate(xs, axis=0)
+            x_ring[new, group(g)] = x
+            h1 = dot(x, w_x2[...]) + jnp.concatenate(parts, axis=0)
             h1s.append(jnp.maximum(h1.astype(BF16), nought))
         return h1s
 
     def variance(cgs):
-        lows = [cgs[u].astype(BF16) for u in us]
-        variances = [dot(lows[u] * lows[u], w_avg2[...]) for u in us]
-        return variances
+        weight = vecs[4:5, 0:LAT]
+        results = []
+        for cg in cgs:
+            halves = []
+            for h in range(2):
+                v = cg[:, h * LAT : (h + 1) * LAT]
+                mean_sq = jnp.sum(v * v * weight, axis=1, keepdims=True)
+                halves.append(jnp.broadcast_to(mean_sq, v.shape))
+            results.append(jnp.concatenate(halves, axis=1))
+        return results
 
     def finish(i, cgs, variances):
         k1, b1, j1 = where_of(i, 1)
         old = lax.rem(i + RING - 1, RING)
-        for u in us:
-            scaled = (cgs[u] * lax.rsqrt(variances[u] + EPS)).astype(BF16) + (x_ring[old, u] + shift)
-            left_count = counts[0, jnp.minimum(b1[u], BANDS - 1)] - j1[u] * BLK
-            for h in range(2):
-                bound = jnp.clip(left_count - h * HALF, 0, HALF).astype(F32)
-                bound = jnp.full((HALF, LAT), bound).astype(BF16)
-                v = jnp.where(slot_id < bound, scaled[:, h * LAT : (h + 1) * LAT], nought)
-                out_v[half_rows(k1[u], h), :] = v
+        for g in groups:
+            scaled = (cgs[g] * lax.rsqrt(variances[g] + EPS)).astype(BF16) + (x_ring[old, group(g)] + shift)
+            for t in range(GROUP):
+                u = g * GROUP + t
+                left_count = counts[0, jnp.minimum(b1[u], BANDS - 1)] - j1[u] * BLK
+                for h in range(2):
+                    bound = jnp.clip(left_count - h * HALF, 0, HALF).astype(F32)
+                    bound = jnp.full((HALF, LAT), bound).astype(BF16)
+                    v = scaled[t * HALF : (t + 1) * HALF, h * LAT : (h + 1) * LAT]
+                    out_v[half_rows(k1[u], h), :] = jnp.where(slot_id < bound, v, nought)
 
     def hidden(h1s):
-        for u in us:
-            h2_s[u] = jnp.maximum(dot(h1s[u], w_hid2[...]).astype(BF16) + bias2, nought)
+        for g in groups:
+            h2_s[group(g)] = jnp.maximum(dot(h1s[g], w_hid2[...]).astype(BF16) + bias2, nought)
 
     def step(i, _):
         scatter(i)
@@ -524,8 +551,8 @@
             pltpu.VMEM((BLK, LAT), BF16),
             pltpu.VMEM((BANDS + 1, BAND_NODES, LAT), F32),
             pltpu.SMEM((TRASH + NB * (2 * STAGES + 2),), jnp.int32),
-            pltpu.VMEM((RING, NB, HALF, 256), BF16),
-            pltpu.VMEM((NB, HALF, 256), BF16),
+            pltpu.VMEM((RING, NB * HALF, 256), BF16),
+            pltpu.VMEM((NB * HALF, 256), BF16),
             pltpu.VMEM((ROWS * COLS, LAT), BF16),
             pltpu.SemaphoreType.DMA,
             pltpu.SemaphoreType.DMA((4,)),

time: 31.1 us -> 30.4 us (0.977); the launches traced: 31.2 us -> 30 us
  Pallas kernels: 30.5 us -> 29.3 us
    pallas_call x1, Pallas kernels: 19.9 us -> 18.8 us  [exchange(): pl.pallas_call(exchange_kernel, out_shape=outs, in_specs=[hbm] * (3 + N_S...]
where the time goes in v5:
time: 30.4 us; the launch traced here: 30 us
  Pallas kernels  29.3 us (96%)
  between operations  0.66 us (2%)
    pallas_call x1, Pallas kernels, exchange(): pl.pallas_call(exchange_kernel, out_shape=outs, in_specs=[hbm] * (3 + N_S...  18.8 us
    pallas_call x1, Pallas kernels, process(): pl.pallas_call(main_kernel, out_shape=(jax.ShapeDtypeStruct((ROWS * COLS,...  10.6 us

profile of v5, /device:TPU:1, one launch (start us, length us, event | category | flops | bytes accessed | tf_op | source)
XLA Modules:
  0.0 30.0 jit_solution(393390664839957243)
XLA Ops:
  0.6 0.0 copy-start
  0.6 18.8 %exchange.1 = (f32[8,128]{1,0:T(8,128)S(1)}, bf16[16640,128]{1,0:T(8,128)(2,1)S(1)}, f32[16640,128]{1,0:T(8,128)S(1)}, bf16[64,32,128]{2,1,0:T(8,128)(2,1)S(1)},...) custom-call(bf16[64,32,128]{2,1,0:T(8,128)(2,1)} %refs_0_.1, ...), custom_call_target="tpu_custom_call" | custom-call | tf_op jit(solution)/shard_map/exchange/pallas_call | solution.py:337
  19.4 0.0 copy-done
  19.4 10.6 %process.1 = (bf16[2048,128]{1,0:T(8,128)(2,1)}, bf16[16384,128]{1,0:T(8,128)(2,1)}) custom-call(s32[1,16]{1,0:T(1,128)S(1)} %bitcast.11, f32[8,128]{1,0:T(8,128)S(1)} %get-tuple-element.19.stats, bf16[16640,128]{1,0:T(8,128)(2,1)S(1)} %get-tuple-element.20.edges_v, f32[16640,128]{1,0:T(8,128)S(1)} %get-tuple-element.21.part_v, ...), custom_call_target="tpu_custom_call" | custom-call | tf_op jit(solution)/shard_map/process/pallas_call | solution.py:541
Async XLA Ops:
  0.6 18.8 %copy-start = (s32[1,1,16]{2,1,0:T(1,128)S(1)}, s32[1,1,16]{2,1,0:T(1,128)}, u32[]{:S(2)}) copy-start(s32[1,1,16]{2,1,0:T(1,128)} %param.21) | copy-start | bytes 196
